TPU v7x, 32 devices: a whole 2x2x4 slice. The times are simulated.
32 devices in a mesh: grp: 16 (over z, y, x), loc: 2 (over core).
Axes of the slice: x: 2, y: 2, z: 4, core: 2. Of those that a mesh axis runs over, the one named last changes fastest.
Arguments:
- tokens: bfloat16 [1024, 3584], P(('grp', 'loc')), may hold values from -6 to 6
- gate_weights: bfloat16 [1024, 8], P(('grp', 'loc')), may hold values from 0.099609375 to 0.59765625
- expert_ids: int32 [1024, 8], P(('grp', 'loc')), may hold values from 0 to 31, as said below
- w_gate: bfloat16 [32, 3584, 1024], P('grp', None, 'loc'), may hold values from -0.09375 to 0.09375
- w_up: bfloat16 [32, 3584, 1024], P('grp', None, 'loc'), may hold values from -0.09375 to 0.09375
- w_down: bfloat16 [32, 3584, 1024], P('grp', None, 'loc'), may hold values from -0.1875 to 0.1875
Outputs:
- layer_out: bfloat16 [1024, 3584], P(('grp', 'loc'))
Inputs may be any that keep to these rules, and one draw needn't show every extreme that they name: `expert_ids`: each row names 8 different experts: two in each of 4 different routing groups, a routing group being 4 consecutive expert numbers. Among the rows of one device (aligned blocks of 32 rows) each expert is named at most 16 times, and in every such block some expert is named exactly 16 times.
All inputs are finite; a program needn't handle non-finite values.
Results may differ from a plain program's by a relative error of at most 0.01.
Values may be sent and summed in bfloat16 or wider, within the bound.
A program may use at most 192 MiB of HBM per device.

v0:
```python
import functools

import jax
import jax.numpy as jnp
from jax import lax
from jax.experimental import pallas as pl
from jax.experimental.pallas import tpu as pltpu
from jax.sharding import PartitionSpec as P

RGROUPS = 8
LANES = 128
MESH = pl.DeviceIdType.MESH


class Place:
    def __init__(self, columns):
        self.deep = columns // 4
        self.g = lax.axis_index("grp")
        self.c = lax.axis_index("loc")
        self.x = lax.rem(self.g, 2)
        self.y = lax.rem(lax.div(self.g, 2), 2)
        self.z = lax.div(self.g, 4)
        self.below = self.z > 0
        self.above = self.z < self.deep - 1

    def at(self, dz=0, fx=0, fy=0):
        x = 1 - self.x if fx else self.x
        y = 1 - self.y if fy else self.y
        return (self.z + dz) * 4 + y * 2 + x

    def line(self, step):
        if step == 0:
            return [(0, None)]
        return [(-step, self.z >= step), (step, self.z + step < self.deep)]


def when(cond, act):
    if cond is None:
        act()
    else:
        pl.when(cond)(act)


def greet(me):
    barrier = pltpu.get_barrier_semaphore()
    partners = [
        (None, me.at(fx=1), me.c),
        (None, me.at(fy=1), me.c),
        (None, me.g, 1 - me.c),
        (me.below, me.at(dz=-1), me.c),
        (me.above, me.at(dz=1), me.c),
    ]
    for cond, g, c in partners:
        when(cond, lambda g=g, c=c: pl.semaphore_signal(
            barrier, inc=1, device_id=(g, c), device_id_type=MESH))
    edges = (me.z > 0).astype(jnp.int32) + (me.z < me.deep - 1).astype(jnp.int32)
    pl.semaphore_wait(barrier, 3 + edges)


def gather_kernel(columns, own_ref, out_ref, own_sem, send_sem, ici_sem, loc_sem):
    me = Place(columns)
    rows = own_ref.shape[0]
    half = rows // 2
    greet(me)

    def slot(h, g, c):
        return out_ref.at[pl.ds(pl.multiple_of((g * 2 + c) * rows + h * half, half), half)]

    base = pl.multiple_of((me.g * 2 + me.c) * rows, rows)
    keep = pltpu.make_async_copy(own_ref, out_ref.at[pl.ds(base, rows)], own_sem)
    keep.start()
    sends = []

    def push(cond, h, g, kind, device, own):
        source = own_ref.at[pl.ds(h * half, half)] if own else slot(h, g, me.c)
        arrive = loc_sem if kind == 4 else ici_sem
        copy = pltpu.make_async_remote_copy(
            src_ref=source, dst_ref=slot(h, g, me.c),
            send_sem=send_sem.at[h, g, kind], recv_sem=arrive.at[h, g],
            device_id=device, device_id_type=MESH)
        when(cond, copy.start)
        sends.append((cond, copy))

    def arrived(cond, h, g):
        copy = pltpu.make_async_remote_copy(
            src_ref=slot(h, g, me.c), dst_ref=slot(h, g, me.c),
            send_sem=send_sem.at[h, g, 0], recv_sem=ici_sem.at[h, g],
            device_id=(me.g, 1 - me.c), device_id_type=MESH)
        when(cond, copy.wait_recv)

    def both(a, b):
        return b if a is None else jnp.logical_and(a, b)

    flips = [dict(fx=1), dict(fy=1)]

    def first(step):
        for dz, cond in me.line(step):
            for h in range(2):
                g = me.at(dz)
                if step:
                    arrived(cond, h, g)
                if dz <= 0:
                    push(both(cond, me.above), h, g, 0, (me.at(1), me.c), step == 0)
                if dz >= 0:
                    push(both(cond, me.below), h, g, 1, (me.at(-1), me.c), step == 0)
                push(cond, h, g, 2, (me.at(**flips[h]), me.c), step == 0)
                push(cond, h, g, 3, (me.at(**flips[1 - h]), me.c), step == 0)
                push(cond, h, g, 4, (me.g, 1 - me.c), step == 0)

    def second(step):
        for dz, cond in me.line(step):
            for h in range(2):
                g = me.at(dz, **flips[h])
                arrived(cond, h, g)
                push(cond, h, g, 3, (me.at(**flips[1 - h]), me.c), False)
                push(cond, h, g, 4, (me.g, 1 - me.c), False)

    def third(step):
        for dz, cond in me.line(step):
            for h in range(2):
                for g in (me.at(dz, **flips[1 - h]), me.at(dz, fx=1, fy=1)):
                    arrived(cond, h, g)
                    push(cond, h, g, 4, (me.g, 1 - me.c), False)

    for turn in range(me.deep + 2):
        for stage, lag in ((first, 0), (second, 1), (third, 2)):
            if 0 <= turn - lag < me.deep:
                stage(turn - lag)
    for h in range(2):
        for g in range(columns):
            pltpu.make_async_remote_copy(
                src_ref=slot(h, g, 1 - me.c), dst_ref=slot(h, g, 1 - me.c),
                send_sem=send_sem.at[h, g, 4], recv_sem=loc_sem.at[h, g],
                device_id=(me.g, 1 - me.c), device_id_type=MESH).wait_recv()
    for cond, copy in sends:
        when(cond, copy.wait_send)
    keep.wait()


def gather_tokens(joined, columns):
    rows, width = joined.shape
    dma = pltpu.SemaphoreType.DMA
    return pl.pallas_call(
        functools.partial(gather_kernel, columns),
        out_shape=jax.ShapeDtypeStruct((columns * 2 * rows, width), joined.dtype),
        in_specs=[pl.BlockSpec(memory_space=pltpu.VMEM)],
        out_specs=pl.BlockSpec(memory_space=pltpu.VMEM),
        scratch_shapes=[dma, dma((2, columns, 5)), dma((2, columns)), dma((2, columns))],
        compiler_params=pltpu.CompilerParams(
            collective_id=1, has_side_effects=True, vmem_limit_bytes=24 * 2**20),
        name="gather_tokens",
    )(joined)


def scatter_kernel(columns, part_ref, out_ref, sums, from_loc, from_two, from_one, from_low,
                   from_high, loc_send, send_sem, loc_sem, two_sem, one_sem, low_sem, high_sem):
    me = Place(columns)
    rows = out_ref.shape[0]
    half = rows // 2
    width = out_ref.shape[1]
    piece = width // 4 if width % (4 * LANES) == 0 else width
    greet(me)
    flips = [dict(fx=1), dict(fy=1)]
    sends = []

    def start(h, g):
        return pl.multiple_of((g * 2 + me.c) * rows + h * half, half)

    def to_core(h, g, cond):
        base = pl.multiple_of((g * 2 + 1 - me.c) * rows + h * half, half)
        copy = pltpu.make_async_remote_copy(
            src_ref=part_ref.at[pl.ds(base, half)], dst_ref=from_loc.at[h, g],
            send_sem=loc_send.at[h, g], recv_sem=loc_sem.at[h, g],
            device_id=(me.g, 1 - me.c), device_id_type=MESH)
        when(cond, copy.start)
        sends.append((cond, copy))

    def send(cond, h, g, buffer, sem, device):
        copy = pltpu.make_async_remote_copy(
            src_ref=sums.at[h, g], dst_ref=buffer.at[h, g],
            send_sem=send_sem.at[h, g], recv_sem=sem.at[h, g],
            device_id=device, device_id_type=MESH)
        when(cond, copy.start)
        sends.append((cond, copy))

    def add(h, g, terms, final=False):
        for buffer, sem in terms:
            pltpu.make_async_remote_copy(
                src_ref=buffer.at[h, g], dst_ref=buffer.at[h, g],
                send_sem=send_sem.at[h, g], recv_sem=sem.at[h, g],
                device_id=(me.g, 1 - me.c), device_id_type=MESH).wait_recv()
        for low in range(0, width, piece):
            cols = slice(low, low + piece)
            total = part_ref[pl.ds(start(h, g), half), cols].astype(jnp.float32)
            for buffer, _ in terms:
                total = total + buffer[h, g, :, cols].astype(jnp.float32)
            if final:
                out_ref[h * half:(h + 1) * half, cols] = total.astype(out_ref.dtype)
            else:
                sums[h, g, :, cols] = total.astype(sums.dtype)

    loc, two, one = (from_loc, loc_sem), (from_two, two_sem), (from_one, one_sem)
    low, high = (from_low, low_sem), (from_high, high_sem)

    def third(step, act):
        for h in range(2):
            for dz, cond in me.line(step):
                for g in (me.at(dz, fx=1, fy=1), me.at(dz, **flips[1 - h])):
                    act(h, g, cond)

    def second(step, act):
        for h in range(2):
            for dz, cond in me.line(step):
                act(h, me.at(dz, **flips[h]), cond)

    def first(step, act):
        for h in range(2):
            for dz, cond in me.line(step):
                act(h, me.at(dz), cond, dz)

    steps = range(me.deep - 1, -1, -1)
    for step in steps:
        third(step, to_core)
    for step in steps:
        second(step, to_core)
        first(step, lambda h, g, cond, dz: to_core(h, g, cond))

    def cross_two(h, g, cond):
        when(cond, lambda: add(h, g, [loc]))
        send(cond, h, g, from_two, two_sem, (me.at(**flips[1 - h]), me.c))

    def cross_one(h, g, cond):
        when(cond, lambda: add(h, g, [loc, two]))
        send(cond, h, g, from_one, one_sem, (me.at(**flips[h]), me.c))

    def cross_line(h, g, cond, dz):
        if dz > 0:
            edge, near, away = me.below, low, me.at(1)
        elif dz < 0:
            edge, near, away = me.above, high, me.at(-1)
        else:
            for under in (False, True):
                for over in (False, True):
                    if me.deep == 1 and (under or over):
                        continue
                    fits = jnp.logical_and(me.below == under, me.above == over)
                    terms = [loc, two, one] + [low] * under + [high] * over
                    pl.when(fits)(lambda terms=terms: add(h, g, terms, True))
            return
        pl.when(jnp.logical_and(cond, edge))(lambda: add(h, g, [loc, two, one, near]))
        inner = jnp.logical_and(cond, jnp.logical_not(edge))
        pl.when(inner)(lambda: add(h, g, [loc, two, one]))
        target = low if dz > 0 else high
        send(cond, h, g, target[0], target[1], (away, me.c))

    for turn in range(me.deep + 2):
        for stage, act, lag in ((third, cross_two, 0), (second, cross_one, 1), (first, cross_line, 2)):
            if 0 <= turn - lag < me.deep:
                stage(me.deep - 1 - (turn - lag), act)
    for cond, copy in sends:
        when(cond, copy.wait_send)


def scatter_sums(partial, columns):
    rows = partial.shape[0] // (2 * columns)
    width = partial.shape[1]
    dma = pltpu.SemaphoreType.DMA
    buffer = pltpu.VMEM((2, columns, rows // 2, width), partial.dtype)
    return pl.pallas_call(
        functools.partial(scatter_kernel, columns),
        out_shape=jax.ShapeDtypeStruct((rows, width), partial.dtype),
        in_specs=[pl.BlockSpec(memory_space=pltpu.VMEM)],
        out_specs=pl.BlockSpec(memory_space=pltpu.VMEM),
        scratch_shapes=[buffer] * 6 + [dma((2, columns))] * 7,
        compiler_params=pltpu.CompilerParams(
            collective_id=2, has_side_effects=True, vmem_limit_bytes=34 * 2**20),
        name="scatter_sums",
    )(partial)


def down_kernel(*refs):
    *hidden, down_ref, out_ref = refs
    total = None
    for expert, ref in enumerate(hidden):
        term = lax.dot_general(
            ref[...], down_ref[expert], (((1,), (1,)), ((), ())),
            preferred_element_type=jnp.float32)
        total = term if total is None else total + term
    out_ref[...] = total.astype(out_ref.dtype)


def project_down(hidden, w_down):
    experts, width, units = w_down.shape
    rows = hidden[0].shape[0]
    tile = 512 if width % 512 == 0 else width
    return pl.pallas_call(
        down_kernel,
        grid=(width // tile,),
        out_shape=jax.ShapeDtypeStruct((rows, width), jnp.bfloat16),
        in_specs=[pl.BlockSpec((rows, units), lambda i: (0, 0))] * experts
        + [pl.BlockSpec((experts, tile, units), lambda i: (0, i, 0))],
        out_specs=pl.BlockSpec((rows, tile), lambda i: (0, i)),
        compiler_params=pltpu.CompilerParams(vmem_limit_bytes=24 * 2**20),
        name="project_down",
    )(*hidden, w_down)


def dense_body(tokens, gate_weights, expert_ids, w_gate, w_up, w_down):
    width = tokens.shape[1]
    local_experts = w_gate.shape[0]
    columns = lax.axis_size("grp")
    expert_total = columns * local_experts
    padded = -(-expert_total // LANES) * LANES
    numbers = jnp.arange(padded, dtype=jnp.int32)
    chosen = expert_ids[:, :, None] == numbers[None, None, :]
    table = jnp.sum(
        jnp.where(chosen, gate_weights.astype(jnp.float32)[:, :, None], 0.0), axis=1
    ).astype(jnp.bfloat16)
    gathered = gather_tokens(jnp.concatenate([tokens, table], axis=1), columns)
    rows = gathered[:, :width]
    first = width + lax.axis_index("grp") * local_experts
    scales = lax.dynamic_slice_in_dim(gathered, first, local_experts, axis=1).astype(jnp.float32)
    hidden = []
    for expert in range(local_experts):
        gate_act = lax.optimization_barrier(
            jnp.dot(rows, w_gate[expert], preferred_element_type=jnp.float32))
        upward = jnp.dot(rows, w_up[expert], preferred_element_type=jnp.float32)
        value = jax.nn.silu(gate_act) * upward * scales[:, expert : expert + 1]
        hidden.append(value.astype(jnp.bfloat16))
    partial = project_down(lax.optimization_barrier(tuple(hidden)), w_down)
    return scatter_sums(partial, columns)


def expert_rows(inputs, scales, gate_part, up_part, down_part):
    gate_act = jnp.dot(inputs, gate_part, preferred_element_type=jnp.float32)
    upward = jnp.dot(inputs, up_part, preferred_element_type=jnp.float32)
    hidden = (jax.nn.silu(gate_act) * upward).astype(jnp.bfloat16)
    projected = lax.dot_general(
        hidden, down_part, (((1,), (1,)), ((), ())), preferred_element_type=jnp.float32
    )
    return projected * scales.astype(jnp.float32)[:, None]


def weights_path(rows_in, scales_in, w_gate, w_up, w_down):
    row_dims = rows_in.shape
    shard_units = w_gate.shape[2]
    expert_inputs = [rows_in[:, expert].reshape(-1, row_dims[3]) for expert in range(row_dims[1])]
    expert_scales = [scales_in[:, expert].reshape(-1) for expert in range(row_dims[1])]
    starting = tuple(
        (
            jnp.zeros((row_dims[0] * row_dims[2], row_dims[3]), jnp.float32)
            for expert in range(row_dims[1])
        )
    )
    gate_piece = lax.all_gather(w_gate, "loc", axis=2, tiled=True)
    up_piece = lax.all_gather(w_up, "loc", axis=2, tiled=True)
    down_piece = lax.all_gather(w_down, "loc", axis=2, tiled=True)
    updated = []
    for expert in range(row_dims[1]):
        running = starting[expert]
        for block_index in range(gate_piece.shape[2] // shard_units):
            lower_unit = block_index * shard_units
            upper_unit = lower_unit + shard_units
            values = expert_rows(
                expert_inputs[expert],
                expert_scales[expert],
                gate_piece[expert][:, lower_unit:upper_unit],
                up_piece[expert][:, lower_unit:upper_unit],
                down_piece[expert][:, lower_unit:upper_unit],
            )
            rounded = lax.optimization_barrier(values.astype(jnp.bfloat16))
            running = running + rounded.astype(jnp.float32)
        updated.append(running)
    folded = tuple(updated)
    stacked = jnp.stack(
        [folded_part.reshape(row_dims[0], row_dims[2], row_dims[3]) for folded_part in folded],
        axis=1,
    )
    return stacked.astype(jnp.bfloat16)


def slot_body(tokens, gate_weights, expert_ids, w_gate, w_up, w_down):
    tok_count = tokens.shape[0]
    choices_per = expert_ids.shape[1]
    feature_count = tokens.shape[1]
    group_count = lax.axis_size("grp")
    local_experts = w_gate.shape[0]
    expert_total = group_count * local_experts
    slot_depth = 2 * tok_count * RGROUPS // expert_total
    slot_total = expert_total * slot_depth
    pair_ids = expert_ids.reshape(-1)
    pair_count = pair_ids.shape[0]
    pair_order = jnp.arange(pair_count, dtype=jnp.int32)
    same_expert = (pair_ids[:, None] == pair_ids[None, :]).astype(jnp.int32)
    earlier = (pair_order[:, None] > pair_order[None, :]).astype(jnp.int32)
    slot_rank = jnp.sum(same_expert * earlier, axis=1)
    position = pair_ids * slot_depth + slot_rank
    pair_onehot = jnp.arange(slot_total, dtype=jnp.int32)[:, None] == position[None, :]
    placement = jnp.sum(
        pair_onehot.reshape(slot_total, tok_count, choices_per).astype(jnp.int32), axis=2
    ).astype(jnp.bfloat16)
    send_rows = jnp.dot(placement, tokens, preferred_element_type=jnp.float32).astype(jnp.bfloat16)
    flat_scales = gate_weights.reshape(-1).astype(jnp.float32)
    send_scales = jnp.sum(jnp.where(pair_onehot, flat_scales[None, :], 0.0), axis=1).astype(
        jnp.bfloat16
    )
    send_rows = send_rows.reshape(group_count, local_experts, slot_depth, feature_count)
    send_scales = send_scales.reshape(group_count, local_experts, slot_depth)
    computed = weights_path(
        lax.all_to_all(send_rows, "grp", split_axis=0, concat_axis=0, tiled=True),
        lax.all_to_all(send_scales, "grp", split_axis=0, concat_axis=0, tiled=True),
        w_gate,
        w_up,
        w_down,
    )
    returned = lax.all_to_all(computed, "grp", split_axis=0, concat_axis=0, tiled=True)
    flat_back = returned.reshape(slot_total, feature_count)
    mixed_out = lax.dot_general(
        placement, flat_back, (((0,), (0,)), ((), ())), preferred_element_type=jnp.float32
    )
    return mixed_out.astype(jnp.bfloat16)


def body(tokens, gate_weights, expert_ids, w_gate, w_up, w_down):
    tok_count = tokens.shape[0]
    columns = lax.axis_size("grp")
    slot_depth = 2 * tok_count * RGROUPS // (columns * w_gate.shape[0])
    dense = slot_depth * w_gate.shape[0] >= tok_count
    fits = columns % 4 == 0 and lax.axis_size("loc") == 2 and tok_count % 32 == 0
    chosen = dense_body if dense and fits else slot_body
    return chosen(tokens, gate_weights, expert_ids, w_gate, w_up, w_down)


def solution(mesh):
    placed = (
        P(("grp", "loc"), None),
        P(("grp", "loc"), None),
        P(("grp", "loc"), None),
        P("grp", None, "loc"),
        P("grp", None, "loc"),
        P("grp", None, "loc"),
    )
    return jax.shard_map(
        body, mesh=mesh, in_specs=placed, out_specs=P(("grp", "loc"), None), check_vma=False
    )
```

profile of v0, /device:TPU:0, one launch (start us, length us, event | category | flops | bytes accessed | tf_op | source)
XLA Modules:
  0.0 111.5 jit_solution(14701702670843163688)
XLA Ops:
  0.0 0.8 copy.12
  0.8 0.8 copy.11
  1.5 0.1 select_reduce_fusion
  1.7 1.0 pad_maximum_fusion.own_ref
  2.6 0.0 copy-start
  2.6 39.7 %gather_tokens.1 = bf16[1024,3712]{1,0:T(8,128)(2,1)S(1)} custom-call(bf16[32,3712]{1,0:T(8,128)(2,1)S(1)} %pad_maximum_fusion.own_ref), custom_call_target="tpu_custom_call" | custom-call | tf_op jit(solution)/shard_map/gather_tokens/pallas_call | solution.py:143
  42.4 0.1 dynamic-slice_convert_fusion
  42.5 0.0 slice-start.2
  42.5 0.5 slice_reduce_fusion
  43.0 0.0 copy-done
  43.1 0.0 slice-start.3
  43.1 3.9 %fusion.2 = f32[1024,512]{1,0:T(8,128)S(1)} fusion(bf16[1024,3712]{1,0:T(8,128)(2,1)S(1)} %gather_tokens.1, bf16[2,3584,512]{2,1,0:T(8,128)(2,1)S(1)} %copy-done), kind=kOutput, calls=%fused_computation.2 | convolution fusion | flops 3758096384 | bytes 13107200 | tf_op jit(solution)/shard_map/dot_general | solution.py:326
  47.0 0.0 slice-done.2
  47.0 0.0 slice-done.3
  47.0 4.2 %multiply_convert_fusion.refs_1_ = bf16[1024,512]{1,0:T(8,128)(2,1)S(1)} fusion(f32[1024,512]{1,0:T(8,128)S(1)} %fusion.2, bf16[2,3584,512]{2,1,0:T(8,128)(2,1)S(1)} %bitcast.19, bf16[1024,3712]{1,0:T(8,128)(2,1)S(1)} %gather_tokens.1, f32[1024]{0:T(1024)S(1)} %get-tuple-element.9), kind=kOutput, calls=%fused_computation.16 | convolution fusion | flops 3761766400 | bytes 14159872 | tf_op jit(solution)/shard_map/dot_general | solution.py:327
  51.2 0.0 slice-start
  51.2 3.9 %fusion.6 = f32[1024,512]{1,0:T(8,128)S(1)} fusion(bf16[1024,3712]{1,0:T(8,128)(2,1)S(1)} %gather_tokens.1, bf16[2,3584,512]{2,1,0:T(8,128)(2,1)S(1)} %copy-done), kind=kOutput, calls=%fused_computation.6 | convolution fusion | flops 3758096384 | bytes 13107200 | tf_op jit(solution)/shard_map/dot_general | solution.py:326
  55.2 0.0 slice-start.1
  55.2 6.4 %multiply_convert_fusion.1.refs_0_ = bf16[1024,512]{1,0:T(8,128)(2,1)S(1)} fusion(f32[1024,512]{1,0:T(8,128)S(1)} %fusion.6, bf16[2,3584,512]{2,1,0:T(8,128)(2,1)} %param.10, bf16[1024,3712]{1,0:T(8,128)(2,1)S(1)} %gather_tokens.1, f32[1024]{0:T(1024)S(1)} %get-tuple-element.10), kind=kOutput, calls=%fused_computation.17 | convolution fusion | flops 3761766400 | bytes 14159872 | tf_op jit(solution)/shard_map/dot_general | solution.py:327
  61.6 0.0 slice-done
  61.6 0.0 slice-done.1
  61.6 9.9 %project_down.1.part_ref = bf16[1024,3584]{1,0:T(8,128)(2,1)S(1)} custom-call(bf16[1024,512]{1,0:T(8,128)(2,1)S(1)} %multiply_convert_fusion.1.refs_0_, bf16[1024,512]{1,0:T(8,128)(2,1)S(1)} %multiply_convert_fusion.refs_1_, bf16[2,3584,512]{2,1,0:T(8,128)(2,1)S(1)} %bitcast.17), custom_call_target="tpu_custom_call" | custom-call | tf_op jit(solution)/shard_map/project_down/pallas_call | solution.py:296
  71.5 39.2 %scatter_sums.1 = bf16[32,3584]{1,0:T(8,128)(2,1)S(1)} custom-call(bf16[1024,3584]{1,0:T(8,128)(2,1)S(1)} %project_down.1.part_ref), custom_call_target="tpu_custom_call" | custom-call | tf_op jit(solution)/shard_map/scatter_sums/pallas_call | solution.py:269
  110.8 0.7 copy.14
  (2 shorter events, 0.0 us)
Async XLA Ops:
  2.6 40.4 %copy-start = (bf16[2,3584,512]{2,1,0:T(8,128)(2,1)S(1)}, bf16[2,3584,512]{2,1,0:T(8,128)(2,1)}, u32[]{:S(2)}) copy-start(bf16[2,3584,512]{2,1,0:T(8,128)(2,1)} %param.9) | copy-start | bytes 22020100
  42.5 4.5 %slice-start.2 = ((s8[7340032]{0:T(1024)(128)(4,1)}), s8[4194304]{0:T(1024)(128)(4,1)S(1)}, s32[]{:S(2)}) async-start(s8[7340032]{0:T(1024)(128)(4,1)} %bitcast.18), calls=%async_computation.2 | async-start | bytes 8388608
  43.1 4.0 %slice-start.3 = ((s8[7340032]{0:T(1024)(128)(4,1)}), s8[3145728]{0:T(1024)(128)(4,1)S(1)}, s32[]{:S(2)}) async-start(s8[7340032]{0:T(1024)(128)(4,1)} %bitcast.18), calls=%async_computation.3 | async-start | bytes 6291456
  51.2 10.4 %slice-start = ((s8[7340032]{0:T(1024)(128)(4,1)}), s8[4194304]{0:T(1024)(128)(4,1)S(1)}, s32[]{:S(2)}) async-start(s8[7340032]{0:T(1024)(128)(4,1)} %bitcast.16), calls=%async_computation | async-start | bytes 8388608
  55.2 6.4 %slice-start.1 = ((s8[7340032]{0:T(1024)(128)(4,1)}), s8[3145728]{0:T(1024)(128)(4,1)S(1)}, s32[]{:S(2)}) async-start(s8[7340032]{0:T(1024)(128)(4,1)} %bitcast.16), calls=%async_computation.1 | async-start | bytes 6291456
where the time goes:
time: 112 us; the launch traced here: 111 us
  Pallas kernels  88.9 us (79%)
  matrix products  18.5 us (17%)
  local copies, waits for them, and re-layouts  2.74 us (2%)
  other arithmetic  1.25 us (1%)
    pallas_call x1, Pallas kernels, gather_tokens(): pl.pallas_call(functools.partial(gather_kernel, columns), out_shape=jax.S...  39.7 us
    pallas_call x1, Pallas kernels, scatter_sums(): pl.pallas_call(functools.partial(scatter_kernel, columns), out_shape=jax....  39.2 us
    dot_general x2, matrix products, dense_body(): upward = jnp.dot(rows, w_up[expert], preferred_element_type=jnp.float32)  10.6 us
    pallas_call x1, Pallas kernels, project_down(): pl.pallas_call(down_kernel, grid=(width // tile,), out_shape=jax.ShapeDty...  9.9 us
    dot_general x2, matrix products, dense_body(): jnp.dot(rows, w_gate[expert], preferred_element_type=jnp.float32)  7.87 us

commit v1 on v0

v1 whole, which is shorter than its diff:
```python
import functools

import jax
import jax.numpy as jnp
from jax import lax
from jax.experimental import pallas as pl
from jax.experimental.pallas import tpu as pltpu
from jax.sharding import PartitionSpec as P

RGROUPS = 8
LANES = 128
TILE = 256
MESH = pl.DeviceIdType.MESH
FLIPS = ((1, 0), (0, 1))
HERE, DIAG = (0, 0), (1, 1)


class Place:
    def __init__(self, columns):
        self.deep = columns // 4
        self.g = lax.axis_index("grp")
        self.c = lax.axis_index("loc")
        self.x = lax.rem(self.g, 2)
        self.y = lax.rem(lax.div(self.g, 2), 2)
        self.z = lax.div(self.g, 4)
        self.below = self.z > 0
        self.above = self.z < self.deep - 1

    def spot(self, flip):
        x = 1 - self.x if flip[0] else self.x
        y = 1 - self.y if flip[1] else self.y
        return y * 2 + x

    def at(self, dz=0, flip=HERE):
        return (self.z + dz) * 4 + self.spot(flip)

    def line(self, step):
        if step == 0:
            return [(0, None)]
        return [(-step, self.z >= step), (step, self.z + step < self.deep)]

    def layer(self, order):
        picked = self.z
        for z in range(self.deep):
            ranked = sorted(range(self.deep), key=lambda other: (abs(other - z), other))
            picked = jnp.where(self.z == z, ranked[order], picked)
        return picked


def when(cond, act):
    if cond is None:
        act()
    else:
        pl.when(cond)(act)


def both(a, b):
    return b if a is None else jnp.logical_and(a, b)


def greet(me):
    barrier = pltpu.get_barrier_semaphore()
    partners = [
        (None, me.at(0, (1, 0)), me.c),
        (None, me.at(0, (0, 1)), me.c),
        (None, me.g, 1 - me.c),
        (me.below, me.at(-1), me.c),
        (me.above, me.at(1), me.c),
    ]
    for cond, g, c in partners:
        when(cond, lambda g=g, c=c: pl.semaphore_signal(
            barrier, inc=1, device_id=(g, c), device_id_type=MESH))
    edges = (me.z > 0).astype(jnp.int32) + (me.z < me.deep - 1).astype(jnp.int32)
    pl.semaphore_wait(barrier, 3 + edges)


def layer_kernel(columns, split, tiles, tokens_hbm, ids_ref, gains_ref, wg_hbm, wu_hbm, wd_hbm, out_ref,
                 rows_ref, wg, wu, wd, hid, part, mine, two, one, low, high,
                 own_sem, weight_sem, gz_send, gz_ici, gz_loc, gc_send, gc_ici, gc_half, gc_loc,
                 sl_send, sl_recv, sz_send, two_sem, one_sem, low_sem, high_sem,
                 sc_send, sx_send, xtwo_sem, xone_sem, clow_sem, chigh_sem):
    me = Place(columns)
    deep = me.deep
    rows, width = tokens_hbm.shape
    half = rows // 2
    lot = 8 * rows
    experts, _, units = wd.shape
    blocks = units // TILE
    lines = [me.line(step) for step in range(deep)]
    layers = [me.layer(order) for order in range(deep)]
    front, rest = slice(0, split), slice(split, width)
    carried = slice(split, rows_ref.shape[1])
    spots = (HERE,) + FLIPS + (DIAG,)
    sends = []

    own_rows = pl.multiple_of((me.z * 8 + me.c * 4 + me.spot(HERE)) * rows, rows)
    own_copy = pltpu.make_async_copy(
        tokens_hbm, rows_ref.at[pl.ds(own_rows, rows), 0:width], own_sem)
    own_copy.start()
    weight_copies = []
    for s in range(experts * blocks):
        e, n = divmod(s, blocks)
        for kind, (source, target) in enumerate(((wg_hbm, wg), (wu_hbm, wu))):
            weight_copies.append(pltpu.make_async_copy(
                source.at[e, :, n * TILE:(n + 1) * TILE], target.at[s], weight_sem.at[kind, s]))
    for e in range(experts):
        weight_copies.append(pltpu.make_async_copy(wd_hbm.at[e], wd.at[e], weight_sem.at[2, e]))
    for copy in weight_copies:
        copy.start()
    numbers = lax.broadcasted_iota(jnp.int32, (rows, rows_ref.shape[1] - width), 1)
    table = jnp.zeros(numbers.shape, jnp.float32)
    gains = gains_ref[...].astype(jnp.float32)
    ids = ids_ref[...]
    for k in range(ids.shape[1]):
        table = table + jnp.where(ids[:, k:k + 1] == numbers, gains[:, k:k + 1], 0.0)
    rows_ref[pl.ds(own_rows, rows), width:] = table.astype(rows_ref.dtype)
    greet(me)

    def row(c, dz=0, flip=HERE, h=0):
        return pl.multiple_of(((me.z + dz) * 8 + c * 4 + me.spot(flip)) * rows + h * half, half)

    def post(dz=0, flip=HERE, h=0):
        return pl.multiple_of(((me.z + dz) * 4 + me.spot(flip)) * rows + h * half, half)

    def device(kind, h=0):
        return {
            "up": lambda: (me.at(1), me.c),
            "down": lambda: (me.at(-1), me.c),
            "near": lambda: (me.at(0, FLIPS[h]), me.c),
            "side": lambda: (me.at(0, FLIPS[1 - h]), me.c),
            "core": lambda: (me.g, 1 - me.c),
        }[kind]()

    def remote(source, target, send_sem, recv_sem, where):
        return pltpu.make_async_remote_copy(
            src_ref=source, dst_ref=target, send_sem=send_sem, recv_sem=recv_sem,
            device_id=where, device_id_type=MESH)

    def issue(cond, make):
        when(cond(), lambda: make().start())
        sends.append((cond, make))

    def landed(ref, sem):
        remote(ref, ref, own_sem, sem, (me.g, 1 - me.c)).wait_recv()

    ALWAYS = lambda: None
    SLOT = {"up": 0, "down": 1, "near": 2, "side": 3, "core": 4}

    def z_slot(h, dz, flip):
        return rows_ref.at[pl.ds(row(me.c, dz, flip, h), half), carried]

    def push_z(cond, h, dz, flip, kind):
        def make():
            g = me.at(dz, flip)
            slot = z_slot(h, dz, flip)
            recv = gz_loc if kind == "core" else gz_ici
            return remote(slot, slot, gz_send.at[h, g, SLOT[kind]], recv.at[h, g], device(kind, h))
        issue(cond, make)

    def z_landed(cond, h, dz, flip):
        when(cond, lambda: landed(z_slot(h, dz, flip), gz_ici.at[h, me.at(dz, flip)]))

    def c_slot(dz, flip, h=None):
        size = rows if h is None else half
        return rows_ref.at[pl.ds(row(me.c, dz, flip, h or 0), size), front]

    def push_c(cond, dz, flip, kind, h=None, k=0):
        def make():
            g = me.at(dz, flip)
            slot = c_slot(dz, flip, h)
            recv = gc_loc.at[g] if kind == "core" else gc_ici.at[g] if h is None else gc_half.at[h]
            return remote(slot, slot, gc_send.at[g, SLOT[kind]], recv, device(kind, k))
        issue(cond, make)

    def z_first(step):
        for dz, cond in lines[step]:
            for h in range(2):
                if step:
                    z_landed(cond, h, dz, HERE)
                if dz <= 0:
                    push_z(lambda cond=cond: both(cond, me.above), h, dz, HERE, "up")
                if dz >= 0:
                    push_z(lambda cond=cond: both(cond, me.below), h, dz, HERE, "down")
                push_z(lambda cond=cond: cond, h, dz, HERE, "near")
            for h in range(2):
                push_z(lambda cond=cond: cond, h, dz, HERE, "side")
                push_z(lambda cond=cond: cond, h, dz, HERE, "core")

    def z_second(step):
        for dz, cond in lines[step]:
            for h in range(2):
                z_landed(cond, h, dz, FLIPS[h])
                push_z(lambda cond=cond: cond, h, dz, FLIPS[h], "side")
                push_z(lambda cond=cond: cond, h, dz, FLIPS[h], "core")

    def z_third(step):
        for dz, cond in lines[step]:
            for h in range(2):
                for flip in (FLIPS[1 - h], DIAG):
                    z_landed(cond, h, dz, flip)
                    push_z(lambda cond=cond: cond, h, dz, flip, "core")

    def along(flip):
        push_c(lambda: me.above, 0, flip, "up")
        push_c(lambda: me.below, 0, flip, "down")
        push_c(ALWAYS, 0, flip, "core")

    def c_first():
        for k in range(2):
            push_c(ALWAYS, 0, HERE, "near" if k == 0 else "side")
        along(HERE)

    def c_second():
        for k in range(2):
            landed(c_slot(0, FLIPS[k]), gc_ici.at[me.at(0, FLIPS[k])])
            push_c(ALWAYS, 0, FLIPS[k], "side", h=k, k=k)
            along(FLIPS[k])

    def c_third():
        for h in range(2):
            landed(c_slot(0, DIAG, h), gc_half.at[h])
        along(DIAG)

    def c_line(step):
        for dz, cond in lines[step]:
            for flip in spots:
                when(cond, lambda: landed(c_slot(dz, flip), gc_ici.at[me.at(dz, flip)]))
                if dz < 0:
                    push_c(lambda cond=cond: both(cond, me.above), dz, flip, "up")
                else:
                    push_c(lambda cond=cond: both(cond, me.below), dz, flip, "down")
                push_c(lambda cond=cond: cond, dz, flip, "core")

    def other_core(order):
        for spot in range(4):
            g = layers[order] * 4 + spot
            base = pl.multiple_of((layers[order] * 8 + (1 - me.c) * 4 + spot) * rows, rows)
            landed(rows_ref.at[pl.ds(base, rows), front], gc_loc.at[g])
            for h in range(2):
                start = pl.multiple_of(base + h * half, half)
                landed(rows_ref.at[pl.ds(start, half), carried], gz_loc.at[h, g])

    def hidden_step(order, s):
        base = pl.multiple_of(layers[order] * lot, lot)
        e, n = lax.div(s, blocks), lax.rem(s, blocks)
        x = rows_ref[pl.ds(base, lot), 0:width]
        gate = jnp.dot(x, wg[s], preferred_element_type=jnp.float32)
        upward = jnp.dot(x, wu[s], preferred_element_type=jnp.float32)
        scales = rows_ref[pl.ds(base, lot), width:].astype(jnp.float32)
        lane = lax.broadcasted_iota(jnp.int32, scales.shape, 1)
        scale = jnp.sum(jnp.where(lane == me.g * experts + e, scales, 0.0), axis=1, keepdims=True)
        value = jax.nn.silu(gate) * upward * scale
        hid[e, :, pl.ds(pl.multiple_of(n * TILE, TILE), TILE)] = value.astype(hid.dtype)

    def down_step(order, t):
        base = pl.multiple_of(layers[order] * lot, lot)
        cols = slice(*tiles[t])
        total = None
        for e in range(experts):
            term = lax.dot_general(
                hid[e], wd[e, cols, :], (((1,), (1,)), ((), ())), preferred_element_type=jnp.float32)
            total = term if total is None else total + term
        part[pl.ds(base, lot), cols] = total.astype(part.dtype)

        def make():
            start = pl.multiple_of((layers[order] * 8 + (1 - me.c) * 4) * rows, 4 * rows)
            there = pl.multiple_of(layers[order] * 4 * rows, 4 * rows)
            return remote(
                part.at[pl.ds(start, 4 * rows), cols], mine.at[pl.ds(there, 4 * rows), cols],
                sl_send.at[layers[order], t], sl_recv.at[layers[order], t], device("core"))
        issue(ALWAYS, make)

    def add(size, cols, terms, target, start):
        for at in range(cols.start, cols.stop, TILE):
            piece = slice(at, at + TILE)
            total = None
            for ref, base in terms:
                term = ref[pl.ds(base, size), piece].astype(jnp.float32)
                total = term if total is None else total + term
            target[pl.ds(start, size), piece] = total.astype(target.dtype)

    def own_terms(dz, flip, h=0):
        return [(part, row(me.c, dz, flip, h)), (mine, post(dz, flip, h))]

    def from_core(dz, steps):
        start = pl.multiple_of((me.z + dz) * 4 * rows, 4 * rows)
        for t in steps:
            landed(mine.at[pl.ds(start, 4 * rows), slice(*tiles[t])], sl_recv.at[me.z + dz, t])

    def two_at(dz, j, h):
        return pl.multiple_of((((me.z + dz) * 2 + j) * 2 + h) * half, half)

    def one_at(dz, h):
        return pl.multiple_of(((me.z + dz) * 2 + h) * half, half)

    def send_sum(cond, dz, flip, h, size, cols, target, there, send_sem, recv_sem, kind):
        def make():
            return remote(
                mine.at[pl.ds(post(dz, flip, h), size), cols],
                target.at[pl.ds(there(), size), cols], send_sem(), recv_sem(), device(kind, h))
        issue(cond, make)

    def s_third(step):
        for dz, cond in lines[step]:
            when(cond, lambda: from_core(dz, range(1, len(tiles))))
            for h in range(2):
                for j, flip in ((1, DIAG), (0, FLIPS[1 - h])):
                    when(cond, lambda: add(
                        half, rest, own_terms(dz, flip, h), mine, post(dz, flip, h)))
                    send_sum(
                        lambda cond=cond: cond, dz, flip, h, half, rest, two,
                        lambda dz=dz, j=j, h=h: two_at(dz, j, h),
                        lambda dz=dz, flip=flip, h=h: sz_send.at[h, me.at(dz, flip)],
                        lambda dz=dz, j=j, h=h: two_sem.at[me.z + dz, j, h], "side")

    def s_second(step):
        for dz, cond in lines[step]:
            for h in range(2):
                flip = FLIPS[h]

                def act():
                    landed(two.at[pl.ds(two_at(dz, 1, h), half), rest], two_sem.at[me.z + dz, 1, h])
                    add(half, rest, own_terms(dz, flip, h) + [(two, two_at(dz, 1, h))],
                        mine, post(dz, flip, h))
                when(cond, act)
                send_sum(
                    lambda cond=cond: cond, dz, flip, h, half, rest, one,
                    lambda dz=dz, h=h: one_at(dz, h),
                    lambda dz=dz, flip=flip, h=h: sz_send.at[h, me.at(dz, flip)],
                    lambda dz=dz, h=h: one_sem.at[me.z + dz, h], "near")

    def from_line(ref, sem, edge, dz, h):
        at = ref.at[pl.ds(post(dz, HERE, h), half), rest]
        pl.when(edge)(lambda: landed(at, sem.at[me.z + dz, h]))

    def s_first(step):
        for dz, cond in lines[step]:
            for h in range(2):
                def act():
                    landed(two.at[pl.ds(two_at(dz, 0, h), half), rest], two_sem.at[me.z + dz, 0, h])
                    landed(one.at[pl.ds(one_at(dz, h), half), rest], one_sem.at[me.z + dz, h])
                    terms = own_terms(dz, HERE, h) + [(two, two_at(dz, 0, h)), (one, one_at(dz, h))]
                    if dz >= 0:
                        from_line(low, low_sem, me.below, dz, h)
                        terms.append((low, post(dz, HERE, h)))
                    if dz <= 0:
                        from_line(high, high_sem, me.above, dz, h)
                        terms.append((high, post(dz, HERE, h)))
                    if dz == 0:
                        add(half, rest, terms, out_ref, h * half)
                    else:
                        add(half, rest, terms, mine, post(dz, HERE, h))
                when(cond, act)
                if dz:
                    target, sem, kind = (low, low_sem, "up") if dz > 0 else (high, high_sem, "down")
                    send_sum(
                        lambda cond=cond: cond, dz, HERE, h, half, rest, target,
                        lambda dz=dz, h=h: post(dz, HERE, h),
                        lambda dz=dz, h=h: sz_send.at[h, me.at(dz)],
                        lambda dz=dz, h=h, sem=sem: sem.at[me.z + dz, h], kind)

    def c_near(dz, flip):
        g = me.at(dz, flip)
        spot = pl.ds(post(dz, flip), rows)
        if dz >= 0:
            pl.when(me.below)(lambda: landed(low.at[spot, front], clow_sem.at[g]))
        if dz <= 0:
            pl.when(me.above)(lambda: landed(high.at[spot, front], chigh_sem.at[g]))

    def t_line(step):
        for dz, cond in lines[step]:
            when(cond, lambda: from_core(dz, (0,)))
            near, sem, kind = (low, clow_sem, "up") if dz > 0 else (high, chigh_sem, "down")
            for flip in spots:
                def act():
                    c_near(dz, flip)
                    add(rows, front, own_terms(dz, flip) + [(near, post(dz, flip))],
                        mine, post(dz, flip))
                when(cond, act)
                send_sum(
                    lambda cond=cond: cond, dz, flip, 0, rows, front, near,
                    lambda dz=dz, flip=flip: post(dz, flip),
                    lambda dz=dz, flip=flip: sc_send.at[me.at(dz, flip)],
                    lambda dz=dz, flip=flip, sem=sem: sem.at[me.at(dz, flip)], kind)

    def lined(flip, h):
        return own_terms(0, flip, h) + [(low, post(0, flip, h)), (high, post(0, flip, h))]

    def t_third():
        from_core(0, (0,))
        for flip in (DIAG,) + FLIPS + (HERE,):
            c_near(0, flip)
        for h in range(2):
            for j, flip in ((1, DIAG), (0, FLIPS[1 - h])):
                add(half, front, lined(flip, h), mine, post(0, flip, h))
                send_sum(
                    ALWAYS, 0, flip, h, half, front, two, lambda j=j, h=h: two_at(0, j, h),
                    lambda j=j, h=h: sx_send.at[h, j], lambda j=j, h=h: xtwo_sem.at[j, h], "side")

    def t_second():
        for h in range(2):
            flip = FLIPS[h]
            landed(two.at[pl.ds(two_at(0, 1, h), half), front], xtwo_sem.at[1, h])
            add(half, front, lined(flip, h) + [(two, two_at(0, 1, h))], mine, post(0, flip, h))
            send_sum(
                ALWAYS, 0, flip, h, half, front, one, lambda h=h: one_at(0, h),
                lambda h=h: sx_send.at[h, 2], lambda h=h: xone_sem.at[h], "near")

    def t_first():
        for h in range(2):
            landed(two.at[pl.ds(two_at(0, 0, h), half), front], xtwo_sem.at[0, h])
            landed(one.at[pl.ds(one_at(0, h), half), front], xone_sem.at[h])
            add(half, front, lined(HERE, h) + [(two, two_at(0, 0, h)), (one, one_at(0, h))],
                out_ref, h * half)

    def clear(ref):
        def body(i, carry):
            ref[pl.ds(pl.multiple_of(i * half, half), half), :] = jnp.zeros((half, width), ref.dtype)
            return carry
        lax.fori_loop(0, ref.shape[0] // half, body, None)

    last = deep - 1
    own_copy.wait()
    c_first()
    z_first(0)
    c_second()
    pl.when(jnp.logical_not(me.below))(lambda: clear(low))
    pl.when(jnp.logical_not(me.above))(lambda: clear(high))
    gather_steps = gather_plan(deep, dict(
        z_first=z_first, z_second=z_second, z_third=z_third, c_third=c_third, c_line=c_line))
    run(gather_steps[0])
    for copy in weight_copies:
        copy.wait()
    subs = experts * blocks
    for order in range(deep):
        other_core(order)
        acts = gather_steps[1 + order]

        def body(s, carry, order=order, acts=acts):
            for k in range(subs):
                if acts[k]:
                    pl.when(s == k)(lambda k=k: run(acts[k]))
            hidden_step(order, s)
            return carry
        lax.fori_loop(0, subs, body, None)
        for t in range(len(tiles)):
            down_step(order, t)
            if subs + t < len(acts):
                run(acts[subs + t])
    for turn in range(deep + 2):
        for stage, lag in ((s_third, 0), (s_second, 1), (s_first, 2)):
            if 0 <= turn - lag < deep:
                stage(last - (turn - lag))
        if turn < last:
            t_line(last - turn)
        elif turn < deep + 2:
            (t_third, t_second, t_first)[turn - last]()
    for cond, make in sends:
        when(cond(), lambda: make().wait_send())


def run(acts):
    for act in acts:
        act()


def gather_plan(deep, do):
    def act(name, *args):
        return lambda: do[name](*args) if not args or args[0] < deep else None
    before = [act("z_second", 0), act("z_first", 1), act("c_third"), act("z_third", 0)]
    plan = [[[] for _ in range(8)] for _ in range(deep)]
    for order in range(deep):
        step = order + 1
        plan[order][0] += [act("z_second", step), act("c_line", step)]
        plan[order][1] += [act("z_first", step + 1)]
        plan[order][3] += [act("z_third", step)]
    return [before] + plan


def fused_body(tokens, gate_weights, expert_ids, w_gate, w_up, w_down):
    columns = lax.axis_size("grp")
    rows, width = tokens.shape
    experts, _, units = w_gate.shape
    deep = columns // 4
    half = rows // 2
    split = max(1, round(width * 2 / 9 / TILE)) * TILE
    edges = list(range(split, width, 4 * TILE)) + [width]
    tiles = [(0, split)] + list(zip(edges[:-1], edges[1:]))
    padded = -(-columns * experts // LANES) * LANES
    blocks = units // TILE
    bf16 = tokens.dtype
    dma = pltpu.SemaphoreType.DMA
    vmem = lambda *shape: pltpu.VMEM(shape, bf16)
    anywhere = pl.BlockSpec(memory_space=pl.ANY)
    local = pl.BlockSpec(memory_space=pltpu.VMEM)
    lined = columns * rows
    return pl.pallas_call(
        functools.partial(layer_kernel, columns, split, tiles),
        out_shape=jax.ShapeDtypeStruct((rows, width), bf16),
        in_specs=[anywhere, local, local, anywhere, anywhere, anywhere],
        out_specs=local,
        scratch_shapes=[
            vmem(2 * lined, width + padded),
            vmem(experts * blocks, width, TILE), vmem(experts * blocks, width, TILE),
            vmem(experts, width, units),
            vmem(experts, 8 * rows, units),
            vmem(2 * lined, width), vmem(lined, width),
            vmem(deep * 4 * half, width), vmem(deep * rows, width),
            vmem(lined, width), vmem(lined, width),
            dma, dma((3, experts * blocks)),
            dma((2, columns, 5)), dma((2, columns)), dma((2, columns)),
            dma((columns, 5)), dma((columns,)), dma((2,)), dma((columns,)),
            dma((deep, len(tiles))), dma((deep, len(tiles))),
            dma((2, columns)), dma((deep, 2, 2)), dma((deep, 2)), dma((deep, 2)), dma((deep, 2)),
            dma((columns,)), dma((2, 3)), dma((2, 2)), dma((2,)), dma((columns,)), dma((columns,)),
        ],
        compiler_params=pltpu.CompilerParams(
            collective_id=1, has_side_effects=True, vmem_limit_bytes=60 * 2**20),
        name="expert_layer",
    )(tokens, expert_ids, gate_weights, w_gate, w_up, w_down)


def expert_rows(inputs, scales, gate_part, up_part, down_part):
    gate_act = jnp.dot(inputs, gate_part, preferred_element_type=jnp.float32)
    upward = jnp.dot(inputs, up_part, preferred_element_type=jnp.float32)
    hidden = (jax.nn.silu(gate_act) * upward).astype(jnp.bfloat16)
    projected = lax.dot_general(
        hidden, down_part, (((1,), (1,)), ((), ())), preferred_element_type=jnp.float32
    )
    return projected * scales.astype(jnp.float32)[:, None]


def weights_path(rows_in, scales_in, w_gate, w_up, w_down):
    row_dims = rows_in.shape
    shard_units = w_gate.shape[2]
    expert_inputs = [rows_in[:, expert].reshape(-1, row_dims[3]) for expert in range(row_dims[1])]
    expert_scales = [scales_in[:, expert].reshape(-1) for expert in range(row_dims[1])]
    starting = tuple(
        (
            jnp.zeros((row_dims[0] * row_dims[2], row_dims[3]), jnp.float32)
            for expert in range(row_dims[1])
        )
    )
    gate_piece = lax.all_gather(w_gate, "loc", axis=2, tiled=True)
    up_piece = lax.all_gather(w_up, "loc", axis=2, tiled=True)
    down_piece = lax.all_gather(w_down, "loc", axis=2, tiled=True)
    updated = []
    for expert in range(row_dims[1]):
        running = starting[expert]
        for block_index in range(gate_piece.shape[2] // shard_units):
            lower_unit = block_index * shard_units
            upper_unit = lower_unit + shard_units
            values = expert_rows(
                expert_inputs[expert],
                expert_scales[expert],
                gate_piece[expert][:, lower_unit:upper_unit],
                up_piece[expert][:, lower_unit:upper_unit],
                down_piece[expert][:, lower_unit:upper_unit],
            )
            rounded = lax.optimization_barrier(values.astype(jnp.bfloat16))
            running = running + rounded.astype(jnp.float32)
        updated.append(running)
    folded = tuple(updated)
    stacked = jnp.stack(
        [folded_part.reshape(row_dims[0], row_dims[2], row_dims[3]) for folded_part in folded],
        axis=1,
    )
    return stacked.astype(jnp.bfloat16)


def slot_body(tokens, gate_weights, expert_ids, w_gate, w_up, w_down):
    tok_count = tokens.shape[0]
    choices_per = expert_ids.shape[1]
    feature_count = tokens.shape[1]
    group_count = lax.axis_size("grp")
    local_experts = w_gate.shape[0]
    expert_total = group_count * local_experts
    slot_depth = 2 * tok_count * RGROUPS // expert_total
    slot_total = expert_total * slot_depth
    pair_ids = expert_ids.reshape(-1)
    pair_count = pair_ids.shape[0]
    pair_order = jnp.arange(pair_count, dtype=jnp.int32)
    same_expert = (pair_ids[:, None] == pair_ids[None, :]).astype(jnp.int32)
    earlier = (pair_order[:, None] > pair_order[None, :]).astype(jnp.int32)
    slot_rank = jnp.sum(same_expert * earlier, axis=1)
    position = pair_ids * slot_depth + slot_rank
    pair_onehot = jnp.arange(slot_total, dtype=jnp.int32)[:, None] == position[None, :]
    placement = jnp.sum(
        pair_onehot.reshape(slot_total, tok_count, choices_per).astype(jnp.int32), axis=2
    ).astype(jnp.bfloat16)
    send_rows = jnp.dot(placement, tokens, preferred_element_type=jnp.float32).astype(jnp.bfloat16)
    flat_scales = gate_weights.reshape(-1).astype(jnp.float32)
    send_scales = jnp.sum(jnp.where(pair_onehot, flat_scales[None, :], 0.0), axis=1).astype(
        jnp.bfloat16
    )
    send_rows = send_rows.reshape(group_count, local_experts, slot_depth, feature_count)
    send_scales = send_scales.reshape(group_count, local_experts, slot_depth)
    computed = weights_path(
        lax.all_to_all(send_rows, "grp", split_axis=0, concat_axis=0, tiled=True),
        lax.all_to_all(send_scales, "grp", split_axis=0, concat_axis=0, tiled=True),
        w_gate,
        w_up,
        w_down,
    )
    returned = lax.all_to_all(computed, "grp", split_axis=0, concat_axis=0, tiled=True)
    flat_back = returned.reshape(slot_total, feature_count)
    mixed_out = lax.dot_general(
        placement, flat_back, (((0,), (0,)), ((), ())), preferred_element_type=jnp.float32
    )
    return mixed_out.astype(jnp.bfloat16)


def body(tokens, gate_weights, expert_ids, w_gate, w_up, w_down):
    tok_count, width = tokens.shape
    units = w_gate.shape[2]
    columns = lax.axis_size("grp")
    slot_depth = 2 * tok_count * RGROUPS // (columns * w_gate.shape[0])
    dense = slot_depth * w_gate.shape[0] >= tok_count
    fits = (columns % 4 == 0 and lax.axis_size("loc") == 2 and tok_count % 32 == 0
            and width % TILE == 0 and width > TILE and units % TILE == 0)
    chosen = fused_body if dense and fits else slot_body
    return chosen(tokens, gate_weights, expert_ids, w_gate, w_up, w_down)


def solution(mesh):
    placed = (
        P(("grp", "loc"), None),
        P(("grp", "loc"), None),
        P(("grp", "loc"), None),
        P("grp", None, "loc"),
        P("grp", None, "loc"),
        P("grp", None, "loc"),
    )
    return jax.shard_map(
        body, mesh=mesh, in_specs=placed, out_specs=P(("grp", "loc"), None), check_vma=False
    )
```

time: 112 us -> 95 us (0.85)
  matrix products: 18.5 us -> 0 us
  local copies, waits for them, and re-layouts: 2.74 us -> 4.36 us
  Pallas kernels: 88.9 us -> 90.3 us
  other arithmetic: 1.25 us -> 0 us
    dot_general x4 -> x0, matrix products: 18.5 us -> none  [the longest x2 10.6 us: dense_body(): upward = jnp.dot(rows, w_up[expert], preferred_element_type=jnp.float32)]
    unnamed x12 -> x3, local copies, waits for them, and re-layouts: 1.49 us -> 4.36 us
    pallas_call x3 -> x1, Pallas kernels: 88.9 us -> 90.3 us  [fused_body(): pl.pallas_call(functools.partial(layer_kernel, columns, split, tiles), ou...]
where the time goes in v1:
time: 95 us; the launch traced here: 94.6 us
  Pallas kernels  90.3 us (95%)
  local copies, waits for them, and re-layouts  4.36 us (5%)
    pallas_call x1, Pallas kernels, fused_body(): pl.pallas_call(functools.partial(layer_kernel, columns, split, tiles), ou...  90.3 us
    unnamed x3, local copies, waits for them, and re-layouts  4.36 us

profile of v1, /device:TPU:0, one launch (start us, length us, event | category | flops | bytes accessed | tf_op | source)
XLA Modules:
  0.0 94.6 jit_solution(5999946711210736658)
XLA Ops:
  0.0 1.4 %copy.8.gains_ref = bf16[32,8]{1,0:T(8,128)(2,1)} copy(bf16[32,8]{0,1:T(8,128)(2,1)} %param.7) | data formatting | bytes 1024 | tf_op args[1]
  1.4 1.4 %copy.7.ids_ref = s32[32,8]{1,0:T(8,128)} copy(s32[32,8]{0,1:T(8,128)} %param.8) | data formatting | bytes 2048 | tf_op args[2]
  2.7 90.3 %expert_layer.1 = bf16[32,3584]{1,0:T(8,128)(2,1)} custom-call(bf16[32,3584]{1,0:T(8,128)(2,1)} %tokens_hbm.1, s32[32,8]{1,0:T(8,128)} %copy.7.ids_ref, bf16[32,8]{1,0:T(8,128)(2,1)} %copy.8.gains_ref, bf16[2,3584,512]{2,1,0:T(8,128)(2,1)} %wg_hbm.1, bf16[2,3584,512]{2,1,0:T(8,128)(2,1)} %wu_hbm.1, bf16[2,3584,512]{2,1,0:T(8,128)(2,1)} %wd_hbm.1), custom_call_target="tpu_custom_call" | custom-call | tf_op jit(solution)/shard_map/expert_layer/pallas_call | solution.py:497
  93.0 1.6 %copy.10 = bf16[32,3584]{1,0:T(8,128)(2,1)} copy(bf16[32,3584]{1,0:T(8,128)(2,1)} %expert_layer.1) | data formatting | bytes 458752

commit v2 on v1

v2 whole, which is shorter than its diff:
```python
import functools

import jax
import jax.numpy as jnp
from jax import lax
from jax.experimental import pallas as pl
from jax.experimental.pallas import tpu as pltpu
from jax.sharding import PartitionSpec as P

RGROUPS = 8
LANES = 128
TILE = 256
MESH = pl.DeviceIdType.MESH
FLIPS = ((1, 0), (0, 1))
HERE, DIAG = (0, 0), (1, 1)


class Place:
    def __init__(self, columns):
        self.deep = columns // 4
        self.g = lax.axis_index("grp")
        self.c = lax.axis_index("loc")
        self.x = lax.rem(self.g, 2)
        self.y = lax.rem(lax.div(self.g, 2), 2)
        self.z = lax.div(self.g, 4)
        self.below = self.z > 0
        self.above = self.z < self.deep - 1
        self.end = jnp.logical_or(self.z == 0, self.z == self.deep - 1)

    def spot(self, flip):
        x = 1 - self.x if flip[0] else self.x
        y = 1 - self.y if flip[1] else self.y
        return y * 2 + x

    def at(self, dz=0, flip=HERE):
        return (self.z + dz) * 4 + self.spot(flip)

    def line(self, step):
        if step == 0:
            return [(0, None)]
        return [(-step, self.z >= step), (step, self.z + step < self.deep)]

    def layer(self, order):
        picked = self.z
        for z in range(self.deep):
            ranked = sorted(range(self.deep), key=lambda other: (abs(other - z), other))
            picked = jnp.where(self.z == z, ranked[order], picked)
        return picked


def when(cond, act):
    if cond is None:
        act()
    else:
        pl.when(cond)(act)


def both(a, b):
    return b if a is None else jnp.logical_and(a, b)


def greet(me):
    barrier = pltpu.get_barrier_semaphore()
    partners = [
        (None, me.at(0, (1, 0)), me.c),
        (None, me.at(0, (0, 1)), me.c),
        (None, me.g, 1 - me.c),
        (me.below, me.at(-1), me.c),
        (me.above, me.at(1), me.c),
    ]
    for cond, g, c in partners:
        when(cond, lambda g=g, c=c: pl.semaphore_signal(
            barrier, inc=1, device_id=(g, c), device_id_type=MESH))
    edges = (me.z > 0).astype(jnp.int32) + (me.z < me.deep - 1).astype(jnp.int32)
    pl.semaphore_wait(barrier, 3 + edges)


def layer_kernel(columns, split, tiles, tokens_hbm, ids_ref, gains_ref, wg_hbm, wu_hbm, wd_hbm, out_ref,
                 rows_ref, wg, wu, wd, hid, part, mine, two, one, low, high,
                 far, own_sem, weight_sem, down_sem, send_sem, gz_ici, gc_ici, gc_half, core_sem,
                 sum_sem, two_sem, one_sem, low_sem, high_sem, far_sem,
                 xtwo_sem, xone_sem, clow_sem, chigh_sem, cfar_sem):
    me = Place(columns)
    deep = me.deep
    rows, width = tokens_hbm.shape
    half = rows // 2
    lot = 8 * rows
    experts, _, units = wd_hbm.shape
    blocks = units // TILE
    lines = [me.line(step) for step in range(deep)]
    layers = [me.layer(order) for order in range(deep)]
    at_layer = [me.z == layer for layer in range(deep)]
    front, rest = slice(0, split), slice(split, width)
    carried = slice(split, rows_ref.shape[1])
    spots = (HERE,) + FLIPS + (DIAG,)
    sends = {}
    last = deep - 1
    jump = deep > 2

    own_rows = pl.multiple_of((me.z * 8 + me.c * 4 + me.spot(HERE)) * rows, rows)
    own_copy = pltpu.make_async_copy(
        tokens_hbm, rows_ref.at[pl.ds(own_rows, rows), 0:width], own_sem)
    own_copy.start()

    def weights():
        for e in range(experts):
            for b in range(width // units):
                pltpu.make_async_copy(
                    wd_hbm.at[e, b * units:(b + 1) * units, :],
                    wd.at[e * units:(e + 1) * units, b * units:(b + 1) * units], down_sem.at[e]).start()
        for s in range(experts * blocks):
            e, n = divmod(s, blocks)
            for kind, (source, target) in enumerate(((wg_hbm, wg), (wu_hbm, wu))):
                pltpu.make_async_copy(
                    source.at[e, :, n * TILE:(n + 1) * TILE], target.at[s], weight_sem.at[kind]).start()

    numbers = lax.broadcasted_iota(jnp.int32, (rows_ref.shape[1] - width, rows), 0)
    table = jnp.zeros(numbers.shape, jnp.float32)
    gains = gains_ref[...].astype(jnp.float32)
    ids = ids_ref[...]
    for k in range(ids.shape[0]):
        table = table + jnp.where(ids[k:k + 1, :] == numbers, gains[k:k + 1, :], 0.0)
    table = table.astype(rows_ref.dtype)
    unit = (lax.broadcasted_iota(jnp.int32, (rows, rows), 0)
            == lax.broadcasted_iota(jnp.int32, (rows, rows), 1)).astype(rows_ref.dtype)
    rows_ref[pl.ds(own_rows, rows), width:] = lax.dot_general(
        unit, table, (((1,), (1,)), ((), ())), preferred_element_type=jnp.float32).astype(rows_ref.dtype)
    greet(me)

    def row(c, layer, flip=HERE, h=0):
        return pl.multiple_of((layer * 8 + c * 4 + me.spot(flip)) * rows + h * half, half)

    def post(layer, flip=HERE, h=0):
        return pl.multiple_of((layer * 4 + me.spot(flip)) * rows + h * half, half)

    def column(layer, flip=HERE):
        return layer * 4 + me.spot(flip)

    def device(kind, h=0):
        return {
            "up": lambda: (me.at(1), me.c),
            "down": lambda: (me.at(-1), me.c),
            "near": lambda: (me.at(0, FLIPS[h]), me.c),
            "side": lambda: (me.at(0, FLIPS[1 - h]), me.c),
            "core": lambda: (me.g, 1 - me.c),
        }[kind]()

    def remote(source, target, send_sem, recv_sem, where):
        return pltpu.make_async_remote_copy(
            src_ref=source, dst_ref=target, send_sem=send_sem, recv_sem=recv_sem,
            device_id=where, device_id_type=MESH)

    def issue(key, cond, size, cols, make):
        number, _, total, _ = sends.get(key, (len(sends), cond, 0, cols))
        sends[key] = (number, cond, total + size, cols)
        when(cond(), lambda: make(send_sem.at[number]).start())

    def landed(ref, sem):
        remote(ref, ref, own_sem, sem, (me.g, 1 - me.c)).wait_recv()

    def always():
        return None

    def z_slot(h, layer, flip):
        return rows_ref.at[pl.ds(row(me.c, layer, flip, h), half), carried]

    def push_z(key, cond, h, layer, flip, kind):
        def make(sem):
            slot = z_slot(h, layer(), flip)
            recv = core_sem.at[layer()] if kind == "core" else gz_ici.at[h, column(layer(), flip)]
            return remote(slot, slot, sem, recv, device(kind, h))
        issue(key, cond, half, carried, make)

    def z_landed(h, layer, flip):
        landed(z_slot(h, layer, flip), gz_ici.at[h, column(layer, flip)])

    def c_slot(layer, flip, h=None):
        size = rows if h is None else half
        return rows_ref.at[pl.ds(row(me.c, layer, flip, h or 0), size), front]

    def push_c(key, cond, layer, flip, kind, h=None, k=0):
        size = rows if h is None else half

        def make(sem):
            slot = c_slot(layer(), flip, h)
            recv = (core_sem.at[layer()] if kind == "core"
                    else gc_ici.at[column(layer(), flip)] if h is None else gc_half.at[h])
            return remote(slot, slot, sem, recv, device(kind, k))
        issue(key, cond, size, front, make)

    def z_first(step):
        for dz, cond in lines[step]:
            layer = lambda dz=dz: me.z + dz
            for h in range(2):
                if step:
                    when(cond, lambda: z_landed(h, layer(), HERE))
                if dz <= 0 and step < last:
                    push_z(("up", dz), lambda cond=cond: both(cond, me.above), h, layer, HERE, "up")
                if dz >= 0 and step < last:
                    push_z(("down", dz), lambda cond=cond: both(cond, me.below), h, layer, HERE, "down")

    def z_cross(order):
        for kind in ("near", "side", "core"):
            for h in range(2):
                push_z(("cross", order), always, h, lambda: layers[order], HERE, kind)

    def z_second(order):
        for h in range(2):
            z_landed(h, layers[order], FLIPS[h])
            push_z(("second", order), always, h, lambda: layers[order], FLIPS[h], "side")
            push_z(("second", order), always, h, lambda: layers[order], FLIPS[h], "core")

    def z_third(order):
        for flips in (lambda h: FLIPS[1 - h], lambda h: DIAG):
            for h in range(2):
                z_landed(h, layers[order], flips(h))
                push_z(("third", order), always, h, lambda: layers[order], flips(h), "core")

    def own():
        return me.z

    def along(flip):
        push_c("c up", lambda: me.above, own, flip, "up")
        push_c("c down", lambda: me.below, own, flip, "down")
        push_c("c core", always, own, flip, "core")

    def c_first():
        for k in range(2):
            push_c("c first", always, own, HERE, "near" if k == 0 else "side")
        along(HERE)

    def c_second():
        for k in range(2):
            landed(c_slot(me.z, FLIPS[k]), gc_ici.at[me.at(0, FLIPS[k])])
            push_c("c second", always, own, FLIPS[k], "side", h=k, k=k)
            along(FLIPS[k])

    def c_third():
        for h in range(2):
            landed(c_slot(me.z, DIAG, h), gc_half.at[h])
        along(DIAG)

    def c_line(step):
        for dz, cond in lines[step]:
            layer = lambda dz=dz: me.z + dz
            for flip in spots:
                when(cond, lambda: landed(c_slot(layer(), flip), gc_ici.at[column(layer(), flip)]))
                if step < last:
                    edge, kind = (me.above, "up") if dz < 0 else (me.below, "down")
                    push_c(("c on", dz), lambda cond=cond, edge=edge: both(cond, edge), layer, flip, kind)
                push_c(("c in", dz), lambda cond=cond: cond, layer, flip, "core")

    def other_core(order):
        base = pl.multiple_of((layers[order] * 8 + (1 - me.c) * 4) * rows, 4 * rows)
        landed(rows_ref.at[pl.ds(base, 4 * rows), :], core_sem.at[layers[order]])

    def turn_down(e):
        whole = wd.at[e * units:(e + 1) * units, :]
        pltpu.make_async_copy(whole, whole, down_sem.at[e]).wait()
        for b in range(width // units):
            block = (slice(e * units, (e + 1) * units), slice(b * units, (b + 1) * units))
            wd[block] = wd[block].T

    def hidden_step(order, s):
        base = pl.multiple_of(layers[order] * lot, lot)
        e = lax.div(s, blocks)
        x = rows_ref[pl.ds(base, lot), 0:width]
        gate = jnp.dot(x, wg[s], preferred_element_type=jnp.float32)
        upward = jnp.dot(x, wu[s], preferred_element_type=jnp.float32)
        scales = rows_ref[pl.ds(base, lot), width:].astype(jnp.float32)
        lane = lax.broadcasted_iota(jnp.int32, scales.shape, 1)
        scale = jnp.sum(jnp.where(lane == me.g * experts + e, scales, 0.0), axis=1, keepdims=True)
        value = jax.nn.silu(gate) * upward * scale
        hid[:, pl.ds(pl.multiple_of(s * TILE, TILE), TILE)] = value.astype(hid.dtype)

    def down_step(order, t):
        base = pl.multiple_of(layers[order] * lot, lot)
        cols = slice(*tiles[t])
        total = jnp.dot(hid[...], wd[:, cols], preferred_element_type=jnp.float32)
        part[pl.ds(base, lot), cols] = total.astype(part.dtype)

        def make(sem):
            start = pl.multiple_of((layers[order] * 8 + (1 - me.c) * 4) * rows, 4 * rows)
            there = pl.multiple_of(layers[order] * 4 * rows, 4 * rows)
            return remote(
                part.at[pl.ds(start, 4 * rows), cols], mine.at[pl.ds(there, 4 * rows), cols],
                sem, sum_sem.at[layers[order]], device("core"))
        tail = slice(0, width) if t == len(tiles) - 1 else cols
        issue(("part", order), always, 4 * rows if t == len(tiles) - 1 else 0, tail, make)

    def add(size, cols, terms, target, start):
        for at in range(cols.start, cols.stop, TILE):
            piece = slice(at, at + TILE)
            total = None
            for ref, base in terms:
                term = ref[pl.ds(base, size), piece].astype(jnp.float32)
                total = term if total is None else total + term
            target[pl.ds(start, size), piece] = total.astype(target.dtype)

    def own_terms(layer, flip, h=0):
        return [(part, row(me.c, layer, flip, h)), (mine, post(layer, flip, h))]

    def from_core(order):
        start = pl.multiple_of(layers[order] * 4 * rows, 4 * rows)
        landed(mine.at[pl.ds(start, 4 * rows), :], sum_sem.at[layers[order]])

    def two_at(layer, j, h):
        return pl.multiple_of(((layer * 2 + j) * 2 + h) * half, half)

    def one_at(layer, h):
        return pl.multiple_of((layer * 2 + h) * half, half)

    def two_slot(layer, j, h, cols):
        return two.at[pl.ds(two_at(layer, j, h), half), cols]

    def one_slot(layer, h, cols):
        return one.at[pl.ds(one_at(layer, h), half), cols]

    def send_sum(key, cond, layer, flip, h, size, cols, target, recv_sem, where):
        def make(sem):
            return remote(
                mine.at[pl.ds(post(layer(), flip, h), size), cols], target(), sem, recv_sem(), where())
        issue(key, cond, size, cols, make)

    def s_third(order):
        layer = lambda: layers[order]
        from_core(order)
        for j, flips in ((1, lambda h: DIAG), (0, lambda h: FLIPS[1 - h])):
            for h in range(2):
                flip = flips(h)
                add(half, rest, own_terms(layer(), flip, h), mine, post(layer(), flip, h))
                send_sum(
                    ("s third", order), always, layer, flip, h, half, rest,
                    lambda j=j, h=h: two_slot(layer(), j, h, rest),
                    lambda j=j, h=h: two_sem.at[layer(), j, h], lambda h=h: device("side", h))

    def s_second(order):
        layer = lambda: layers[order]
        for h in range(2):
            flip = FLIPS[h]
            landed(two_slot(layer(), 1, h, rest), two_sem.at[layer(), 1, h])
            add(half, rest, own_terms(layer(), flip, h) + [(two, two_at(layer(), 1, h))],
                mine, post(layer(), flip, h))
            send_sum(
                ("s second", order), always, layer, flip, h, half, rest,
                lambda h=h: one_slot(layer(), h, rest), lambda h=h: one_sem.at[layer(), h],
                lambda h=h: device("near", h))

    def columns_in(layer, h):
        landed(two_slot(layer, 0, h, rest), two_sem.at[layer, 0, h])
        landed(one_slot(layer, h, rest), one_sem.at[layer, h])
        return own_terms(layer, HERE, h) + [(two, two_at(layer, 0, h)), (one, one_at(layer, h))]

    def ways(reach, hop):
        for cond, to, name in (
                (at_layer[hop], reach, "up"), (at_layer[deep - 1 - hop], deep - 1 - reach, "down")):
            over = jump and reach == last and hop == 0
            joins = hop > (1 if jump and reach == last else 0)
            near, z_sem, c_sem = (low, low_sem, clow_sem) if name == "up" else (high, high_sem, chigh_sem)
            yield cond, to, name, over, joins, near, z_sem, c_sem

    def z_sum(reach, hop):
        for cond, to, name, over, joins, near, sem, _ in ways(reach, hop):
            for h in range(2):
                def act():
                    terms = columns_in(to, h)
                    if joins:
                        landed(near.at[pl.ds(post(to, HERE, h), half), rest], sem.at[to, h])
                        terms.append((near, post(to, HERE, h)))
                    add(half, rest, terms, mine, post(to, HERE, h))
                pl.when(cond)(act)

                def target(to=to, near=near, over=over, h=h):
                    ref, at = (far, post(0, HERE, h)) if over else (near, post(to, HERE, h))
                    return ref.at[pl.ds(at, half), rest]
                send_sum(
                    ("z sum", name, reach, hop), lambda cond=cond: cond, lambda to=to: to, HERE, h, half,
                    rest, target,
                    lambda to=to, sem=sem, over=over, h=h: far_sem.at[h] if over else sem.at[to, h],
                    lambda to=to, name=name, over=over: (
                        (column(to), me.c) if over else device(name)))

    def c_sum(reach, hop):
        for cond, to, name, over, joins, near, _, sem in ways(reach, hop):
            for flip in spots:
                def act():
                    terms = own_terms(to, flip)
                    if joins:
                        landed(near.at[pl.ds(post(to, flip), rows), front], sem.at[column(to, flip)])
                        terms.append((near, post(to, flip)))
                    add(rows, front, terms, mine, post(to, flip))
                pl.when(cond)(act)

                def target(to=to, near=near, over=over, flip=flip):
                    ref, at = (far, post(0, flip)) if over else (near, post(to, flip))
                    return ref.at[pl.ds(at, rows), front]
                send_sum(
                    ("c sum", name, reach, hop), lambda cond=cond: cond, lambda to=to: to, flip, 0, rows,
                    front, target,
                    lambda to=to, sem=sem, over=over, flip=flip: (
                        cfar_sem.at[me.spot(flip)] if over else sem.at[column(to, flip)]),
                    lambda to=to, name=name, over=over: (
                        (column(to), me.c) if over else device(name)))

    def lined(flip, h):
        beyond = [(low, post(me.z, flip, h)), (high, post(me.z, flip, h))]
        return own_terms(me.z, flip, h) + beyond + ([(far, post(0, flip, h))] if jump else [])

    def z_final():
        for h in range(2):
            terms = columns_in(me.z, h)[2:] + lined(HERE, h)
            spot = pl.ds(post(me.z, HERE, h), half)
            pl.when(me.below)(lambda: landed(low.at[spot, rest], low_sem.at[me.z, h]))
            pl.when(me.above)(lambda: landed(high.at[spot, rest], high_sem.at[me.z, h]))
            if jump:
                spot_far = pl.ds(post(0, HERE, h), half)
                pl.when(me.end)(lambda: landed(far.at[spot_far, rest], far_sem.at[h]))
            add(half, rest, terms, out_ref, h * half)

    def c_back():
        for flip in (DIAG,) + FLIPS + (HERE,):
            g = column(me.z, flip)
            spot = pl.ds(post(me.z, flip), rows)
            pl.when(me.below)(lambda: landed(low.at[spot, front], clow_sem.at[g]))
            pl.when(me.above)(lambda: landed(high.at[spot, front], chigh_sem.at[g]))
            if jump:
                spot_far = pl.ds(post(0, flip), rows)
                pl.when(me.end)(lambda: landed(far.at[spot_far, front], cfar_sem.at[me.spot(flip)]))
        for j, flips in ((1, lambda h: DIAG), (0, lambda h: FLIPS[1 - h])):
            for h in range(2):
                flip = flips(h)
                add(half, front, lined(flip, h), mine, post(me.z, flip, h))
                send_sum(
                    "c back", always, own, flip, h, half, front,
                    lambda j=j, h=h: two_slot(me.z, j, h, front),
                    lambda j=j, h=h: xtwo_sem.at[j, h], lambda h=h: device("side", h))

    def c_cross():
        for h in range(2):
            flip = FLIPS[h]
            landed(two_slot(me.z, 1, h, front), xtwo_sem.at[1, h])
            add(half, front, lined(flip, h) + [(two, two_at(me.z, 1, h))], mine, post(me.z, flip, h))
            send_sum(
                "c cross", always, own, flip, h, half, front, lambda h=h: one_slot(me.z, h, front),
                lambda h=h: xone_sem.at[h], lambda h=h: device("near", h))

    def c_final():
        for h in range(2):
            landed(two_slot(me.z, 0, h, front), xtwo_sem.at[0, h])
            landed(one_slot(me.z, h, front), xone_sem.at[h])
            add(half, front, lined(HERE, h) + [(two, two_at(me.z, 0, h)), (one, one_at(me.z, h))],
                out_ref, h * half)

    def clear(ref, layer):
        base = layer * 4 * rows

        def body(i, carry):
            ref[pl.ds(pl.multiple_of(base + i * half, half), half), :] = jnp.zeros((half, width), ref.dtype)
            return carry
        lax.fori_loop(0, 8, body, None)

    do = dict(
        z_first=z_first, z_cross=z_cross, z_second=z_second, z_third=z_third, c_first=c_first, c_second=c_second,
        c_third=c_third, c_line=c_line, turn_down=turn_down, s_third=s_third, s_second=s_second,
        z_sum=z_sum, c_sum=c_sum, z_final=z_final, c_back=c_back, c_cross=c_cross, c_final=c_final,
        weights=weights,
        clear_low=lambda: pl.when(jnp.logical_not(me.below))(lambda: clear(low, me.z)),
        clear_high=lambda: pl.when(jnp.logical_not(me.above))(lambda: clear(high, me.z)),
        clear_far=lambda: pl.when(jnp.logical_not(me.end))(lambda: clear(far, 0)))
    before, plan, after = order_of_work(deep, experts)

    def run(acts):
        for name, *args in acts:
            do[name](*args)

    own_copy.wait()
    run(before)
    for kind, ref in enumerate((wg, wu)):
        pltpu.make_async_copy(ref, ref, weight_sem.at[kind]).wait()
    subs = experts * blocks
    for order in range(deep):
        other_core(order)
        acts = plan[order]

        def body(s, carry, order=order, acts=acts):
            for k in range(subs):
                if acts.get(k):
                    pl.when(s == k)(lambda k=k: run(acts[k]))
            hidden_step(order, s)
            return carry
        lax.fori_loop(0, subs, body, None)
        for t in range(len(tiles)):
            run(acts.get(subs + t, []))
            down_step(order, t)
    run(after)
    assert len(sends) == send_sem.shape[0], len(sends)
    for number, cond, total, cols in sends.values():
        spent = rows_ref.at[pl.ds(0, total), cols]
        when(cond(), lambda: remote(
            spent, spent, send_sem.at[number], own_sem, (me.g, 1 - me.c)).wait_send())


def order_of_work(deep, experts):
    last = deep - 1
    before = [("c_first",), ("z_first", 0), ("z_cross", 0), ("weights",)]
    before += [("clear_low",), ("clear_high",), ("clear_far",)]
    before += [("c_second",), ("turn_down", 0)]
    before += [("z_second", 0), ("z_first", 1), ("z_cross", 1)]
    before += [("turn_down", e) for e in range(1, experts)]
    before += [("c_third",), ("z_third", 0)]
    plan = [{} for _ in range(deep)]

    def put(order, step, *acts):
        plan[min(order, last)].setdefault(step, []).extend(acts)

    put(0, 1, ("z_second", 1))
    for order in range(last):
        if order:
            put(order, 0, ("z_second", order + 1))
        if order + 2 < deep:
            put(order, 1 if order else 2, ("z_first", order + 2), ("z_cross", order + 2))
        put(order, (2, 4, 4)[order] if deep == 4 else 2, ("c_line", order + 1))
        put(order, 5, ("z_third", order + 1))
    if last > 1:
        put(last - 1, 1, ("s_third", 1), ("c_sum", 1, 0))
        put(last, 0, ("s_second", 1))
        for order in range(2, last):
            put(last, 1, ("s_third", order), ("c_sum", order, 0))
        put(last, 5, ("z_sum", 1, 0))
        for order in range(2, last):
            put(last, 7, ("s_second", order))
    after = [("s_third", last), ("c_sum", last, 0)]
    after += [("c_sum", last, hop) for hop in range(1, 2 if last > 1 else 1)]
    after += [("c_sum", reach, hop) for reach in range(2, last) for hop in range(1, reach)]
    after += [("z_sum", reach, 0) for reach in range(2, last)]
    after += [("s_second", last), ("s_third", 0)]
    after += [("z_sum", last, 0)]
    after += [("z_sum", last, hop) for hop in range(1, 2 if last > 1 else 1)]
    after += [("c_sum", last, hop) for hop in range(2, last)]
    after += [("z_sum", reach, hop) for reach in range(2, last) for hop in range(1, reach)]
    after += [("s_second", 0)]
    after += [("c_back",)]
    after += [("z_sum", last, hop) for hop in range(2, last)]
    after += [("c_cross",), ("z_final",), ("c_final",)]
    return before, plan, after


def fused_body(tokens, gate_weights, expert_ids, w_gate, w_up, w_down):
    columns = lax.axis_size("grp")
    rows, width = tokens.shape
    experts, _, units = w_gate.shape
    deep = columns // 4
    half = rows // 2
    split = max(1, round(width * 2 / 9 / TILE)) * TILE
    edges = list(range(0, width, 4 * TILE)) + [width]
    tiles = list(zip(edges[:-1], edges[1:]))
    padded = -(-columns * experts // LANES) * LANES
    blocks = units // TILE
    bf16 = tokens.dtype
    dma = pltpu.SemaphoreType.DMA
    vmem = lambda *shape: pltpu.VMEM(shape, bf16)
    anywhere = pl.BlockSpec(memory_space=pl.ANY)
    local = pl.BlockSpec(memory_space=pltpu.VMEM)
    lined = columns * rows
    groups = 2 * (deep - 1) + 3 * deep + 5 + 2 * (deep - 1) + 2 * (deep - 2) + 3 * deep + 2 * deep * (deep - 1) + 2
    return pl.pallas_call(
        functools.partial(layer_kernel, columns, split, tiles),
        out_shape=jax.ShapeDtypeStruct((rows, width), bf16),
        in_specs=[anywhere, local, local, anywhere, anywhere, anywhere],
        out_specs=local,
        scratch_shapes=[
            vmem(2 * lined, width + padded),
            vmem(experts * blocks, width, TILE), vmem(experts * blocks, width, TILE),
            vmem(experts * units, width),
            vmem(8 * rows, experts * units),
            vmem(2 * lined, width), vmem(lined, width),
            vmem(deep * 4 * half, width), vmem(deep * rows, width),
            vmem(lined, width), vmem(lined, width),
            vmem(4 * rows, width),
            dma, dma((2,)), dma((experts,)), dma((groups,)), dma((2, columns)), dma((columns,)), dma((2,)),
            dma((deep,)), dma((deep,)), dma((deep, 2, 2)), dma((deep, 2)), dma((deep, 2)), dma((deep, 2)),
            dma((2,)), dma((2, 2)), dma((2,)), dma((columns,)), dma((columns,)), dma((4,)),
        ],
        compiler_params=pltpu.CompilerParams(
            collective_id=1, has_side_effects=True, vmem_limit_bytes=60 * 2**20),
        name="expert_layer",
    )(tokens, expert_ids.T, gate_weights.T, w_gate, w_up, w_down)


def expert_rows(inputs, scales, gate_part, up_part, down_part):
    gate_act = jnp.dot(inputs, gate_part, preferred_element_type=jnp.float32)
    upward = jnp.dot(inputs, up_part, preferred_element_type=jnp.float32)
    hidden = (jax.nn.silu(gate_act) * upward).astype(jnp.bfloat16)
    projected = lax.dot_general(
        hidden, down_part, (((1,), (1,)), ((), ())), preferred_element_type=jnp.float32
    )
    return projected * scales.astype(jnp.float32)[:, None]


def weights_path(rows_in, scales_in, w_gate, w_up, w_down):
    row_dims = rows_in.shape
    shard_units = w_gate.shape[2]
    expert_inputs = [rows_in[:, expert].reshape(-1, row_dims[3]) for expert in range(row_dims[1])]
    expert_scales = [scales_in[:, expert].reshape(-1) for expert in range(row_dims[1])]
    starting = tuple(
        (
            jnp.zeros((row_dims[0] * row_dims[2], row_dims[3]), jnp.float32)
            for expert in range(row_dims[1])
        )
    )
    gate_piece = lax.all_gather(w_gate, "loc", axis=2, tiled=True)
    up_piece = lax.all_gather(w_up, "loc", axis=2, tiled=True)
    down_piece = lax.all_gather(w_down, "loc", axis=2, tiled=True)
    updated = []
    for expert in range(row_dims[1]):
        running = starting[expert]
        for block_index in range(gate_piece.shape[2] // shard_units):
            lower_unit = block_index * shard_units
            upper_unit = lower_unit + shard_units
            values = expert_rows(
                expert_inputs[expert],
                expert_scales[expert],
                gate_piece[expert][:, lower_unit:upper_unit],
                up_piece[expert][:, lower_unit:upper_unit],
                down_piece[expert][:, lower_unit:upper_unit],
            )
            rounded = lax.optimization_barrier(values.astype(jnp.bfloat16))
            running = running + rounded.astype(jnp.float32)
        updated.append(running)
    folded = tuple(updated)
    stacked = jnp.stack(
        [folded_part.reshape(row_dims[0], row_dims[2], row_dims[3]) for folded_part in folded],
        axis=1,
    )
    return stacked.astype(jnp.bfloat16)


def slot_body(tokens, gate_weights, expert_ids, w_gate, w_up, w_down):
    tok_count = tokens.shape[0]
    choices_per = expert_ids.shape[1]
    feature_count = tokens.shape[1]
    group_count = lax.axis_size("grp")
    local_experts = w_gate.shape[0]
    expert_total = group_count * local_experts
    slot_depth = 2 * tok_count * RGROUPS // expert_total
    slot_total = expert_total * slot_depth
    pair_ids = expert_ids.reshape(-1)
    pair_count = pair_ids.shape[0]
    pair_order = jnp.arange(pair_count, dtype=jnp.int32)
    same_expert = (pair_ids[:, None] == pair_ids[None, :]).astype(jnp.int32)
    earlier = (pair_order[:, None] > pair_order[None, :]).astype(jnp.int32)
    slot_rank = jnp.sum(same_expert * earlier, axis=1)
    position = pair_ids * slot_depth + slot_rank
    pair_onehot = jnp.arange(slot_total, dtype=jnp.int32)[:, None] == position[None, :]
    placement = jnp.sum(
        pair_onehot.reshape(slot_total, tok_count, choices_per).astype(jnp.int32), axis=2
    ).astype(jnp.bfloat16)
    send_rows = jnp.dot(placement, tokens, preferred_element_type=jnp.float32).astype(jnp.bfloat16)
    flat_scales = gate_weights.reshape(-1).astype(jnp.float32)
    send_scales = jnp.sum(jnp.where(pair_onehot, flat_scales[None, :], 0.0), axis=1).astype(
        jnp.bfloat16
    )
    send_rows = send_rows.reshape(group_count, local_experts, slot_depth, feature_count)
    send_scales = send_scales.reshape(group_count, local_experts, slot_depth)
    computed = weights_path(
        lax.all_to_all(send_rows, "grp", split_axis=0, concat_axis=0, tiled=True),
        lax.all_to_all(send_scales, "grp", split_axis=0, concat_axis=0, tiled=True),
        w_gate,
        w_up,
        w_down,
    )
    returned = lax.all_to_all(computed, "grp", split_axis=0, concat_axis=0, tiled=True)
    flat_back = returned.reshape(slot_total, feature_count)
    mixed_out = lax.dot_general(
        placement, flat_back, (((0,), (0,)), ((), ())), preferred_element_type=jnp.float32
    )
    return mixed_out.astype(jnp.bfloat16)


def body(tokens, gate_weights, expert_ids, w_gate, w_up, w_down):
    tok_count, width = tokens.shape
    units = w_gate.shape[2]
    columns = lax.axis_size("grp")
    slot_depth = 2 * tok_count * RGROUPS // (columns * w_gate.shape[0])
    dense = slot_depth * w_gate.shape[0] >= tok_count
    fits = (columns % 4 == 0 and lax.axis_size("loc") == 2 and tok_count % 32 == 0
            and columns >= 8 and width % TILE == 0 and width > TILE
            and units % TILE == 0 and width % units == 0)
    chosen = fused_body if dense and fits else slot_body
    return chosen(tokens, gate_weights, expert_ids, w_gate, w_up, w_down)


def solution(mesh):
    placed = (
        P(("grp", "loc"), None),
        P(("grp", "loc"), None),
        P(("grp", "loc"), None),
        P("grp", None, "loc"),
        P("grp", None, "loc"),
        P("grp", None, "loc"),
    )
    return jax.shard_map(
        body, mesh=mesh, in_specs=placed, out_specs=P(("grp", "loc"), None), check_vma=False
    )
```

time: 95 us -> 79.3 us (0.83)
  Pallas kernels: 90.3 us -> 77.4 us
  local copies, waits for them, and re-layouts: 4.36 us -> 1.64 us
    pallas_call x1, Pallas kernels: 90.3 us -> 77.4 us  [fused_body(): pl.pallas_call(functools.partial(layer_kernel, columns, split, tiles), ou...]
    unnamed x3 -> x1, local copies, waits for them, and re-layouts: 4.36 us -> 1.64 us
where the time goes in v2:
time: 79.3 us; the launch traced here: 79.1 us
  Pallas kernels  77.4 us (98%)
  local copies, waits for them, and re-layouts  1.64 us (2%)
    pallas_call x1, Pallas kernels, fused_body(): pl.pallas_call(functools.partial(layer_kernel, columns, split, tiles), ou...  77.4 us
    unnamed x1, local copies, waits for them, and re-layouts  1.64 us

profile of v2, /device:TPU:0, one launch (start us, length us, event | category | flops | bytes accessed | tf_op | source)
XLA Modules:
  0.0 79.1 jit_solution(1965800916986521853)
XLA Ops:
  0.0 77.4 %expert_layer.1 = bf16[32,3584]{1,0:T(8,128)(2,1)} custom-call(bf16[32,3584]{1,0:T(8,128)(2,1)} %tokens_hbm.1, s32[8,32]{1,0:T(8,128)} %bitcast.2, bf16[8,32]{1,0:T(8,128)(2,1)} %bitcast.3, bf16[2,3584,512]{2,1,0:T(8,128)(2,1)} %wg_hbm.1, bf16[2,3584,512]{2,1,0:T(8,128)(2,1)} %wu_hbm.1, bf16[2,3584,512]{2,1,0:T(8,128)(2,1)} %wd_hbm.1), custom_call_target="tpu_custom_call" | custom-call | tf_op jit(solution)/shard_map/expert_layer/pallas_call | solution.py:566
  77.4 1.6 %copy.8 = bf16[32,3584]{1,0:T(8,128)(2,1)} copy(bf16[32,3584]{1,0:T(8,128)(2,1)} %expert_layer.1) | data formatting | bytes 458752

commit v3 on v2

--- a/solution.py
+++ b/solution.py
@@ -75,11 +75,11 @@
     pl.semaphore_wait(barrier, 3 + edges)
 
 
-def layer_kernel(columns, split, tiles, tokens_hbm, ids_ref, gains_ref, wg_hbm, wu_hbm, wd_hbm, out_ref,
-                 rows_ref, wg, wu, wd, hid, part, mine, two, one, low, high,
+def layer_kernel(columns, split, split_back, depth, tiles, tokens_hbm, ids_ref, gains_ref, wg_hbm, wu_hbm, wd_hbm, out_ref,
+                 rows_ref, wg, wu, wd, place, weigh, packed, hid, back, part, mine, two, one, low, high,
                  far, own_sem, weight_sem, down_sem, send_sem, gz_ici, gc_ici, gc_half, core_sem,
                  sum_sem, two_sem, one_sem, low_sem, high_sem, far_sem,
-                 xtwo_sem, xone_sem, clow_sem, chigh_sem, cfar_sem):
+                 xtwo_sem, xone_sem, clow_sem, chigh_sem):
     me = Place(columns)
     deep = me.deep
     rows, width = tokens_hbm.shape
@@ -90,7 +90,8 @@
     lines = [me.line(step) for step in range(deep)]
     layers = [me.layer(order) for order in range(deep)]
     at_layer = [me.z == layer for layer in range(deep)]
-    front, rest = slice(0, split), slice(split, width)
+    direct = slice(0, split)
+    front, rest = slice(0, split_back), slice(split_back, width)
     carried = slice(split, rows_ref.shape[1])
     spots = (HERE,) + FLIPS + (DIAG,)
     sends = {}
@@ -176,7 +177,7 @@
 
     def c_slot(layer, flip, h=None):
         size = rows if h is None else half
-        return rows_ref.at[pl.ds(row(me.c, layer, flip, h or 0), size), front]
+        return rows_ref.at[pl.ds(row(me.c, layer, flip, h or 0), size), direct]
 
     def push_c(key, cond, layer, flip, kind, h=None, k=0):
         size = rows if h is None else half
@@ -186,7 +187,7 @@
             recv = (core_sem.at[layer()] if kind == "core"
                     else gc_ici.at[column(layer(), flip)] if h is None else gc_half.at[h])
             return remote(slot, slot, sem, recv, device(kind, k))
-        issue(key, cond, size, front, make)
+        issue(key, cond, size, direct, make)
 
     def z_first(step):
         for dz, cond in lines[step]:
@@ -202,19 +203,19 @@
     def z_cross(order):
         for kind in ("near", "side", "core"):
             for h in range(2):
-                push_z(("cross", order), always, h, lambda: layers[order], HERE, kind)
+                push_z("z", always, h, lambda: layers[order], HERE, kind)
 
     def z_second(order):
         for h in range(2):
             z_landed(h, layers[order], FLIPS[h])
-            push_z(("second", order), always, h, lambda: layers[order], FLIPS[h], "side")
-            push_z(("second", order), always, h, lambda: layers[order], FLIPS[h], "core")
+            push_z("z", always, h, lambda: layers[order], FLIPS[h], "side")
+            push_z("z", always, h, lambda: layers[order], FLIPS[h], "core")
 
     def z_third(order):
         for flips in (lambda h: FLIPS[1 - h], lambda h: DIAG):
             for h in range(2):
                 z_landed(h, layers[order], flips(h))
-                push_z(("third", order), always, h, lambda: layers[order], flips(h), "core")
+                push_z("z", always, h, lambda: layers[order], flips(h), "core")
 
     def own():
         return me.z
@@ -222,17 +223,17 @@
     def along(flip):
         push_c("c up", lambda: me.above, own, flip, "up")
         push_c("c down", lambda: me.below, own, flip, "down")
-        push_c("c core", always, own, flip, "core")
+        push_c("c", always, own, flip, "core")
 
     def c_first():
         for k in range(2):
-            push_c("c first", always, own, HERE, "near" if k == 0 else "side")
+            push_c("c", always, own, HERE, "near" if k == 0 else "side")
         along(HERE)
 
     def c_second():
         for k in range(2):
             landed(c_slot(me.z, FLIPS[k]), gc_ici.at[me.at(0, FLIPS[k])])
-            push_c("c second", always, own, FLIPS[k], "side", h=k, k=k)
+            push_c("c", always, own, FLIPS[k], "side", h=k, k=k)
             along(FLIPS[k])
 
     def c_third():
@@ -261,23 +262,54 @@
             block = (slice(e * units, (e + 1) * units), slice(b * units, (b + 1) * units))
             wd[block] = wd[block].T
 
+    share = 8 * depth
+
+    def pack(order):
+        base = pl.multiple_of(layers[order] * lot, lot)
+        table = rows_ref[pl.ds(base, lot), width:].astype(jnp.float32)
+        token = lax.broadcasted_iota(jnp.int32, (lot, lot), 0)
+        other = lax.broadcasted_iota(jnp.int32, (lot, lot), 1)
+        earlier = jnp.logical_and(other < token, lax.div(other, rows) == lax.div(token, rows))
+        rank = jnp.dot(
+            jnp.where(earlier, 1.0, 0.0).astype(place.dtype),
+            jnp.where(table > 0.0, 1.0, 0.0).astype(place.dtype), preferred_element_type=jnp.float32)
+        lane = lax.broadcasted_iota(jnp.int32, table.shape, 1)
+        slot = lax.broadcasted_iota(jnp.int32, (lot, share), 1)
+        first = lax.div(lax.broadcasted_iota(jnp.int32, (lot, share), 0), rows) * depth
+        for e in range(experts):
+            pick = lane == me.g * experts + e
+            scale = jnp.sum(jnp.where(pick, table, 0.0), axis=1, keepdims=True)
+            mine_rank = jnp.sum(jnp.where(pick, rank, 0.0), axis=1, keepdims=True)
+            hit = jnp.logical_and((slot - first).astype(jnp.float32) == mine_rank, scale > 0.0)
+            place[:, e * share:(e + 1) * share] = jnp.where(hit, 1.0, 0.0).astype(place.dtype)
+            weigh[:, e * share:(e + 1) * share] = jnp.where(hit, scale, 0.0).astype(weigh.dtype)
+        for cols in tiles:
+            cols = slice(*cols)
+            packed[:, cols] = lax.dot_general(
+                place[...], rows_ref[pl.ds(base, lot), cols], (((0,), (0,)), ((), ())),
+                preferred_element_type=jnp.float32).astype(packed.dtype)
+
     def hidden_step(order, s):
-        base = pl.multiple_of(layers[order] * lot, lot)
-        e = lax.div(s, blocks)
-        x = rows_ref[pl.ds(base, lot), 0:width]
+        del order
+        e, n = lax.div(s, blocks), lax.rem(s, blocks)
+        start = pl.multiple_of(e * share, share)
+        x = packed[pl.ds(start, share), :]
         gate = jnp.dot(x, wg[s], preferred_element_type=jnp.float32)
         upward = jnp.dot(x, wu[s], preferred_element_type=jnp.float32)
-        scales = rows_ref[pl.ds(base, lot), width:].astype(jnp.float32)
-        lane = lax.broadcasted_iota(jnp.int32, scales.shape, 1)
-        scale = jnp.sum(jnp.where(lane == me.g * experts + e, scales, 0.0), axis=1, keepdims=True)
-        value = jax.nn.silu(gate) * upward * scale
-        hid[:, pl.ds(pl.multiple_of(s * TILE, TILE), TILE)] = value.astype(hid.dtype)
+        value = jax.nn.silu(gate) * upward
+        hid[pl.ds(start, share), pl.ds(pl.multiple_of(n * TILE, TILE), TILE)] = value.astype(hid.dtype)
 
     def down_step(order, t):
         base = pl.multiple_of(layers[order] * lot, lot)
         cols = slice(*tiles[t])
-        total = jnp.dot(hid[...], wd[:, cols], preferred_element_type=jnp.float32)
-        part[pl.ds(base, lot), cols] = total.astype(part.dtype)
+        span = slice(0, tiles[t][1] - tiles[t][0])
+        for e in range(experts):
+            mix = slice(e * share, (e + 1) * share)
+            back[mix, span] = jnp.dot(
+                hid[mix, :], wd[e * units:(e + 1) * units, cols],
+                preferred_element_type=jnp.float32).astype(back.dtype)
+        part[pl.ds(base, lot), cols] = jnp.dot(
+            weigh[...], back[:, span], preferred_element_type=jnp.float32).astype(part.dtype)
 
         def make(sem):
             start = pl.multiple_of((layers[order] * 8 + (1 - me.c) * 4) * rows, 4 * rows)
@@ -286,7 +318,7 @@
                 part.at[pl.ds(start, 4 * rows), cols], mine.at[pl.ds(there, 4 * rows), cols],
                 sem, sum_sem.at[layers[order]], device("core"))
         tail = slice(0, width) if t == len(tiles) - 1 else cols
-        issue(("part", order), always, 4 * rows if t == len(tiles) - 1 else 0, tail, make)
+        issue("part", always, 4 * rows if t == len(tiles) - 1 else 0, tail, make)
 
     def add(size, cols, terms, target, start):
         for at in range(cols.start, cols.stop, TILE):
@@ -322,15 +354,18 @@
                 mine.at[pl.ds(post(layer(), flip, h), size), cols], target(), sem, recv_sem(), where())
         issue(key, cond, size, cols, make)
 
-    def s_third(order):
+    def s_third(order, only=None):
         layer = lambda: layers[order]
-        from_core(order)
+        if only != 0:
+            from_core(order)
         for j, flips in ((1, lambda h: DIAG), (0, lambda h: FLIPS[1 - h])):
+            if only not in (None, j):
+                continue
             for h in range(2):
                 flip = flips(h)
                 add(half, rest, own_terms(layer(), flip, h), mine, post(layer(), flip, h))
                 send_sum(
-                    ("s third", order), always, layer, flip, h, half, rest,
+                    "s", always, layer, flip, h, half, rest,
                     lambda j=j, h=h: two_slot(layer(), j, h, rest),
                     lambda j=j, h=h: two_sem.at[layer(), j, h], lambda h=h: device("side", h))
 
@@ -342,7 +377,7 @@
             add(half, rest, own_terms(layer(), flip, h) + [(two, two_at(layer(), 1, h))],
                 mine, post(layer(), flip, h))
             send_sum(
-                ("s second", order), always, layer, flip, h, half, rest,
+                "s", always, layer, flip, h, half, rest,
                 lambda h=h: one_slot(layer(), h, rest), lambda h=h: one_sem.at[layer(), h],
                 lambda h=h: device("near", h))
 
@@ -351,17 +386,17 @@
         landed(one_slot(layer, h, rest), one_sem.at[layer, h])
         return own_terms(layer, HERE, h) + [(two, two_at(layer, 0, h)), (one, one_at(layer, h))]
 
-    def ways(reach, hop):
+    def ways(reach, hop, leap):
         for cond, to, name in (
                 (at_layer[hop], reach, "up"), (at_layer[deep - 1 - hop], deep - 1 - reach, "down")):
-            over = jump and reach == last and hop == 0
-            joins = hop > (1 if jump and reach == last else 0)
+            over = leap and reach == last and hop == 0
+            joins = hop > (1 if leap and reach == last else 0)
             near, z_sem, c_sem = (low, low_sem, clow_sem) if name == "up" else (high, high_sem, chigh_sem)
             yield cond, to, name, over, joins, near, z_sem, c_sem
 
-    def z_sum(reach, hop):
-        for cond, to, name, over, joins, near, sem, _ in ways(reach, hop):
-            for h in range(2):
+    def z_sum(reach, hop, only=None):
+        for h in (0, 1) if only is None else (only,):
+            for cond, to, name, over, joins, near, sem, _ in ways(reach, hop, jump and h == 0):
                 def act():
                     terms = columns_in(to, h)
                     if joins:
@@ -374,14 +409,14 @@
                     ref, at = (far, post(0, HERE, h)) if over else (near, post(to, HERE, h))
                     return ref.at[pl.ds(at, half), rest]
                 send_sum(
-                    ("z sum", name, reach, hop), lambda cond=cond: cond, lambda to=to: to, HERE, h, half,
+                    ("z sum", name, hop), lambda cond=cond: cond, lambda to=to: to, HERE, h, half,
                     rest, target,
                     lambda to=to, sem=sem, over=over, h=h: far_sem.at[h] if over else sem.at[to, h],
                     lambda to=to, name=name, over=over: (
                         (column(to), me.c) if over else device(name)))
 
     def c_sum(reach, hop):
-        for cond, to, name, over, joins, near, _, sem in ways(reach, hop):
+        for cond, to, name, _, joins, near, _, sem in ways(reach, hop, False):
             for flip in spots:
                 def act():
                     terms = own_terms(to, flip)
@@ -390,29 +425,23 @@
                         terms.append((near, post(to, flip)))
                     add(rows, front, terms, mine, post(to, flip))
                 pl.when(cond)(act)
-
-                def target(to=to, near=near, over=over, flip=flip):
-                    ref, at = (far, post(0, flip)) if over else (near, post(to, flip))
-                    return ref.at[pl.ds(at, rows), front]
                 send_sum(
-                    ("c sum", name, reach, hop), lambda cond=cond: cond, lambda to=to: to, flip, 0, rows,
-                    front, target,
-                    lambda to=to, sem=sem, over=over, flip=flip: (
-                        cfar_sem.at[me.spot(flip)] if over else sem.at[column(to, flip)]),
-                    lambda to=to, name=name, over=over: (
-                        (column(to), me.c) if over else device(name)))
-
-    def lined(flip, h):
+                    ("c sum", name, hop), lambda cond=cond: cond, lambda to=to: to, flip, 0, rows, front,
+                    lambda to=to, near=near, flip=flip: near.at[pl.ds(post(to, flip), rows), front],
+                    lambda to=to, sem=sem, flip=flip: sem.at[column(to, flip)],
+                    lambda name=name: device(name))
+
+    def lined(flip, h, leap):
         beyond = [(low, post(me.z, flip, h)), (high, post(me.z, flip, h))]
-        return own_terms(me.z, flip, h) + beyond + ([(far, post(0, flip, h))] if jump else [])
+        return own_terms(me.z, flip, h) + beyond + ([(far, post(0, flip, h))] if leap else [])
 
     def z_final():
         for h in range(2):
-            terms = columns_in(me.z, h)[2:] + lined(HERE, h)
+            terms = columns_in(me.z, h)[2:] + lined(HERE, h, jump and h == 0)
             spot = pl.ds(post(me.z, HERE, h), half)
             pl.when(me.below)(lambda: landed(low.at[spot, rest], low_sem.at[me.z, h]))
             pl.when(me.above)(lambda: landed(high.at[spot, rest], high_sem.at[me.z, h]))
-            if jump:
+            if jump and h == 0:
                 spot_far = pl.ds(post(0, HERE, h), half)
                 pl.when(me.end)(lambda: landed(far.at[spot_far, rest], far_sem.at[h]))
             add(half, rest, terms, out_ref, h * half)
@@ -423,15 +452,12 @@
             spot = pl.ds(post(me.z, flip), rows)
             pl.when(me.below)(lambda: landed(low.at[spot, front], clow_sem.at[g]))
             pl.when(me.above)(lambda: landed(high.at[spot, front], chigh_sem.at[g]))
-            if jump:
-                spot_far = pl.ds(post(0, flip), rows)
-                pl.when(me.end)(lambda: landed(far.at[spot_far, front], cfar_sem.at[me.spot(flip)]))
         for j, flips in ((1, lambda h: DIAG), (0, lambda h: FLIPS[1 - h])):
             for h in range(2):
                 flip = flips(h)
-                add(half, front, lined(flip, h), mine, post(me.z, flip, h))
+                add(half, front, lined(flip, h, False), mine, post(me.z, flip, h))
                 send_sum(
-                    "c back", always, own, flip, h, half, front,
+                    "c sum", always, own, flip, h, half, front,
                     lambda j=j, h=h: two_slot(me.z, j, h, front),
                     lambda j=j, h=h: xtwo_sem.at[j, h], lambda h=h: device("side", h))
 
@@ -439,16 +465,16 @@
         for h in range(2):
             flip = FLIPS[h]
             landed(two_slot(me.z, 1, h, front), xtwo_sem.at[1, h])
-            add(half, front, lined(flip, h) + [(two, two_at(me.z, 1, h))], mine, post(me.z, flip, h))
+            add(half, front, lined(flip, h, False) + [(two, two_at(me.z, 1, h))], mine, post(me.z, flip, h))
             send_sum(
-                "c cross", always, own, flip, h, half, front, lambda h=h: one_slot(me.z, h, front),
+                "c sum", always, own, flip, h, half, front, lambda h=h: one_slot(me.z, h, front),
                 lambda h=h: xone_sem.at[h], lambda h=h: device("near", h))
 
     def c_final():
         for h in range(2):
             landed(two_slot(me.z, 0, h, front), xtwo_sem.at[0, h])
             landed(one_slot(me.z, h, front), xone_sem.at[h])
-            add(half, front, lined(HERE, h) + [(two, two_at(me.z, 0, h)), (one, one_at(me.z, h))],
+            add(half, front, lined(HERE, h, False) + [(two, two_at(me.z, 0, h)), (one, one_at(me.z, h))],
                 out_ref, h * half)
 
     def clear(ref, layer):
@@ -481,6 +507,7 @@
     for order in range(deep):
         other_core(order)
         acts = plan[order]
+        pack(order)
 
         def body(s, carry, order=order, acts=acts):
             for k in range(subs):
@@ -516,31 +543,35 @@
     put(0, 1, ("z_second", 1))
     for order in range(last):
         if order:
-            put(order, 0, ("z_second", order + 1))
+            put(order - 1, 7, ("z_second", order + 1))
         if order + 2 < deep:
-            put(order, 1 if order else 2, ("z_first", order + 2), ("z_cross", order + 2))
-        put(order, (2, 4, 4)[order] if deep == 4 else 2, ("c_line", order + 1))
-        put(order, 5, ("z_third", order + 1))
+            put(order, 0 if order else 2, ("z_first", order + 2), ("z_cross", order + 2))
+        put(order, (2, 5, 4)[order] if deep == 4 else 2, ("c_line", order + 1))
+        put(order, (6, 5, 5)[order] if deep == 4 else 5, ("z_third", order + 1))
     if last > 1:
         put(last - 1, 1, ("s_third", 1), ("c_sum", 1, 0))
+        put(last - 1, 3, ("s_third", 0, 1))
+        put(last, 7, ("z_sum", 1, 0))
         put(last, 0, ("s_second", 1))
         for order in range(2, last):
-            put(last, 1, ("s_third", order), ("c_sum", order, 0))
-        put(last, 5, ("z_sum", 1, 0))
-        for order in range(2, last):
-            put(last, 7, ("s_second", order))
-    after = [("s_third", last), ("c_sum", last, 0)]
+            put(last, 0, ("s_third", order), ("c_sum", order, 0))
+    else:
+        put(last, 0, ("s_third", 0))
+    after = [("s_second", order) for order in range(2, last)]
+    after += [("s_third", last), ("c_sum", last, 0)]
+    after += [("c_sum", reach, hop) for reach in range(2, last) for hop in range(1, reach)]
+    after += [("s_second", last)]
+    if last > 1:
+        after += [("s_third", 0, 0)]
+    after += [("z_sum", reach, 0) for reach in range(2, last)]
     after += [("c_sum", last, hop) for hop in range(1, 2 if last > 1 else 1)]
-    after += [("c_sum", reach, hop) for reach in range(2, last) for hop in range(1, reach)]
-    after += [("z_sum", reach, 0) for reach in range(2, last)]
-    after += [("s_second", last), ("s_third", 0)]
-    after += [("z_sum", last, 0)]
-    after += [("z_sum", last, hop) for hop in range(1, 2 if last > 1 else 1)]
+    after += [("z_sum", last, 0, 1), ("z_sum", last, 0, 0)]
+    after += [("z_sum", last, hop, 0) for hop in range(1, 2 if last > 1 else 1)]
     after += [("c_sum", last, hop) for hop in range(2, last)]
+    after += [("z_sum", last, hop, 1) for hop in range(1, 2 if last > 1 else 1)]
     after += [("z_sum", reach, hop) for reach in range(2, last) for hop in range(1, reach)]
-    after += [("s_second", 0)]
-    after += [("c_back",)]
-    after += [("z_sum", last, hop) for hop in range(2, last)]
+    after += [("s_second", 0), ("c_back",)]
+    after += [("z_sum", last, hop, h) for hop in range(2, last) for h in range(2)]
     after += [("c_cross",), ("z_final",), ("c_final",)]
     return before, plan, after
 
@@ -552,19 +583,21 @@
     deep = columns // 4
     half = rows // 2
     split = max(1, round(width * 2 / 9 / TILE)) * TILE
+    split_back = max(1, round(width / 7 / TILE)) * TILE
     edges = list(range(0, width, 4 * TILE)) + [width]
     tiles = list(zip(edges[:-1], edges[1:]))
     padded = -(-columns * experts // LANES) * LANES
     blocks = units // TILE
     bf16 = tokens.dtype
+    depth = 2 * rows * RGROUPS // (columns * experts)
     dma = pltpu.SemaphoreType.DMA
     vmem = lambda *shape: pltpu.VMEM(shape, bf16)
     anywhere = pl.BlockSpec(memory_space=pl.ANY)
     local = pl.BlockSpec(memory_space=pltpu.VMEM)
     lined = columns * rows
-    groups = 2 * (deep - 1) + 3 * deep + 5 + 2 * (deep - 1) + 2 * (deep - 2) + 3 * deep + 2 * deep * (deep - 1) + 2
+    groups = 8 * (deep - 1) + 2 * (deep - 2) + 7
     return pl.pallas_call(
-        functools.partial(layer_kernel, columns, split, tiles),
+        functools.partial(layer_kernel, columns, split, split_back, depth, tiles),
         out_shape=jax.ShapeDtypeStruct((rows, width), bf16),
         in_specs=[anywhere, local, local, anywhere, anywhere, anywhere],
         out_specs=local,
@@ -572,17 +605,19 @@
             vmem(2 * lined, width + padded),
             vmem(experts * blocks, width, TILE), vmem(experts * blocks, width, TILE),
             vmem(experts * units, width),
-            vmem(8 * rows, experts * units),
+            vmem(8 * rows, experts * 8 * depth), vmem(8 * rows, experts * 8 * depth),
+            vmem(experts * 8 * depth, width), vmem(experts * 8 * depth, units),
+            vmem(experts * 8 * depth, 4 * TILE),
             vmem(2 * lined, width), vmem(lined, width),
             vmem(deep * 4 * half, width), vmem(deep * rows, width),
             vmem(lined, width), vmem(lined, width),
             vmem(4 * rows, width),
             dma, dma((2,)), dma((experts,)), dma((groups,)), dma((2, columns)), dma((columns,)), dma((2,)),
             dma((deep,)), dma((deep,)), dma((deep, 2, 2)), dma((deep, 2)), dma((deep, 2)), dma((deep, 2)),
-            dma((2,)), dma((2, 2)), dma((2,)), dma((columns,)), dma((columns,)), dma((4,)),
+            dma((2,)), dma((2, 2)), dma((2,)), dma((columns,)), dma((columns,)),
         ],
         compiler_params=pltpu.CompilerParams(
-            collective_id=1, has_side_effects=True, vmem_limit_bytes=60 * 2**20),
+            collective_id=1, has_side_effects=True, vmem_limit_bytes=54 * 2**20),
         name="expert_layer",
     )(tokens, expert_ids.T, gate_weights.T, w_gate, w_up, w_down)
 
@@ -685,7 +720,7 @@
     dense = slot_depth * w_gate.shape[0] >= tok_count
     fits = (columns % 4 == 0 and lax.axis_size("loc") == 2 and tok_count % 32 == 0
             and columns >= 8 and width % TILE == 0 and width > TILE
-            and units % TILE == 0 and width % units == 0)
+            and units % TILE == 0 and width % units == 0 and 8 * slot_depth % LANES == 0)
     chosen = fused_body if dense and fits else slot_body
     return chosen(tokens, gate_weights, expert_ids, w_gate, w_up, w_down)
 

time: 79.3 us -> 74.3 us (0.937)
  Pallas kernels: 77.4 us -> 72.4 us
    pallas_call x1, Pallas kernels: 77.4 us -> 72.4 us  [fused_body(): pl.pallas_call(functools.partial(layer_kernel, columns, split, split_back...]
where the time goes in v3:
time: 74.3 us; the launch traced here: 74.1 us
  Pallas kernels  72.4 us (97%)
  local copies, waits for them, and re-layouts  1.64 us (2%)
    pallas_call x1, Pallas kernels, fused_body(): pl.pallas_call(functools.partial(layer_kernel, columns, split, split_back...  72.4 us
    unnamed x1, local copies, waits for them, and re-layouts  1.64 us

profile of v3, /device:TPU:0, one launch (start us, length us, event | category | flops | bytes accessed | tf_op | source)
XLA Modules:
  0.0 74.1 jit_solution(1063833627645922017)
XLA Ops:
  0.0 72.4 %expert_layer.1 = bf16[32,3584]{1,0:T(8,128)(2,1)} custom-call(bf16[32,3584]{1,0:T(8,128)(2,1)} %tokens_hbm.1, s32[8,32]{1,0:T(8,128)} %bitcast.2, bf16[8,32]{1,0:T(8,128)(2,1)} %bitcast.3, bf16[2,3584,512]{2,1,0:T(8,128)(2,1)} %wg_hbm.1, bf16[2,3584,512]{2,1,0:T(8,128)(2,1)} %wu_hbm.1, bf16[2,3584,512]{2,1,0:T(8,128)(2,1)} %wd_hbm.1), custom_call_target="tpu_custom_call" | custom-call | tf_op jit(solution)/shard_map/expert_layer/pallas_call | solution.py:599
  72.4 1.6 %copy.8 = bf16[32,3584]{1,0:T(8,128)(2,1)} copy(bf16[32,3584]{1,0:T(8,128)(2,1)} %expert_layer.1) | data formatting | bytes 458752

commit v4 on v3

--- a/solution.py
+++ b/solution.py
@@ -507,6 +507,7 @@
     for order in range(deep):
         other_core(order)
         acts = plan[order]
+        run(acts.get(-1, []))
         pack(order)
 
         def body(s, carry, order=order, acts=acts):
@@ -543,31 +544,33 @@
     put(0, 1, ("z_second", 1))
     for order in range(last):
         if order:
-            put(order - 1, 7, ("z_second", order + 1))
+            put(*((1, -1) if order == 1 else (order - 1, 7)), ("z_second", order + 1))
         if order + 2 < deep:
             put(order, 0 if order else 2, ("z_first", order + 2), ("z_cross", order + 2))
         put(order, (2, 5, 4)[order] if deep == 4 else 2, ("c_line", order + 1))
         put(order, (6, 5, 5)[order] if deep == 4 else 5, ("z_third", order + 1))
     if last > 1:
-        put(last - 1, 1, ("s_third", 1), ("c_sum", 1, 0))
-        put(last - 1, 3, ("s_third", 0, 1))
-        put(last, 7, ("z_sum", 1, 0))
-        put(last, 0, ("s_second", 1))
+        put(last - 1, 0, ("s_third", 1), ("c_sum", 1, 0))
+        for order in range(2, last):
+            put(last, 7, ("s_second", order))
+        put(last, 7, ("z_sum", 1, 0, 0))
+        put(last, -1, ("s_second", 1))
         for order in range(2, last):
             put(last, 0, ("s_third", order), ("c_sum", order, 0))
     else:
         put(last, 0, ("s_third", 0))
-    after = [("s_second", order) for order in range(2, last)]
-    after += [("s_third", last), ("c_sum", last, 0)]
+    after = [("s_third", last), ("c_sum", last, 0)]
     after += [("c_sum", reach, hop) for reach in range(2, last) for hop in range(1, reach)]
+    after += [("c_sum", last, hop) for hop in range(1, 2 if last > 1 else 1)]
     after += [("s_second", last)]
     if last > 1:
-        after += [("s_third", 0, 0)]
+        after += [("s_third", 0)]
     after += [("z_sum", reach, 0) for reach in range(2, last)]
-    after += [("c_sum", last, hop) for hop in range(1, 2 if last > 1 else 1)]
     after += [("z_sum", last, 0, 1), ("z_sum", last, 0, 0)]
+    if last > 1:
+        after += [("z_sum", 1, 0, 1)]
+    after += [("c_sum", last, hop) for hop in range(2, last)]
     after += [("z_sum", last, hop, 0) for hop in range(1, 2 if last > 1 else 1)]
-    after += [("c_sum", last, hop) for hop in range(2, last)]
     after += [("z_sum", last, hop, 1) for hop in range(1, 2 if last > 1 else 1)]
     after += [("z_sum", reach, hop) for reach in range(2, last) for hop in range(1, reach)]
     after += [("s_second", 0), ("c_back",)]
@@ -583,7 +586,7 @@
     deep = columns // 4
     half = rows // 2
     split = max(1, round(width * 2 / 9 / TILE)) * TILE
-    split_back = max(1, round(width / 7 / TILE)) * TILE
+    split_back = split
     edges = list(range(0, width, 4 * TILE)) + [width]
     tiles = list(zip(edges[:-1], edges[1:]))
     padded = -(-columns * experts // LANES) * LANES

time: 74.3 us -> 72.8 us (0.980)
  Pallas kernels: 72.4 us -> 70.9 us
    pallas_call x1, Pallas kernels: 72.4 us -> 70.9 us  [fused_body(): pl.pallas_call(functools.partial(layer_kernel, columns, split, split_back...]
where the time goes in v4:
time: 72.8 us; the launch traced here: 72.6 us
  Pallas kernels  70.9 us (97%)
  local copies, waits for them, and re-layouts  1.64 us (2%)
    pallas_call x1, Pallas kernels, fused_body(): pl.pallas_call(functools.partial(layer_kernel, columns, split, split_back...  70.9 us
    unnamed x1, local copies, waits for them, and re-layouts  1.64 us

profile of v4, /device:TPU:0, one launch (start us, length us, event | category | flops | bytes accessed | tf_op | source)
XLA Modules:
  0.0 72.6 jit_solution(8470777966852358467)
XLA Ops:
  0.0 70.9 %expert_layer.1 = bf16[32,3584]{1,0:T(8,128)(2,1)} custom-call(bf16[32,3584]{1,0:T(8,128)(2,1)} %tokens_hbm.1, s32[8,32]{1,0:T(8,128)} %bitcast.2, bf16[8,32]{1,0:T(8,128)(2,1)} %bitcast.3, bf16[2,3584,512]{2,1,0:T(8,128)(2,1)} %wg_hbm.1, bf16[2,3584,512]{2,1,0:T(8,128)(2,1)} %wu_hbm.1, bf16[2,3584,512]{2,1,0:T(8,128)(2,1)} %wd_hbm.1), custom_call_target="tpu_custom_call" | custom-call | tf_op jit(solution)/shard_map/expert_layer/pallas_call | solution.py:602
  70.9 1.6 %copy.8 = bf16[32,3584]{1,0:T(8,128)(2,1)} copy(bf16[32,3584]{1,0:T(8,128)(2,1)} %expert_layer.1) | data formatting | bytes 458752

commit v5 on v4

--- a/solution.py
+++ b/solution.py
@@ -348,11 +348,11 @@
     def one_slot(layer, h, cols):
         return one.at[pl.ds(one_at(layer, h), half), cols]
 
-    def send_sum(key, cond, layer, flip, h, size, cols, target, recv_sem, where):
+    def send_sum(key, cond, layer, flip, h, size, cols, target, recv_sem, where, spent=None):
         def make(sem):
             return remote(
                 mine.at[pl.ds(post(layer(), flip, h), size), cols], target(), sem, recv_sem(), where())
-        issue(key, cond, size, cols, make)
+        issue(key, cond, *(spent or (size, cols)), make)
 
     def s_third(order, only=None):
         layer = lambda: layers[order]
@@ -381,9 +381,10 @@
                 lambda h=h: one_slot(layer(), h, rest), lambda h=h: one_sem.at[layer(), h],
                 lambda h=h: device("near", h))
 
-    def columns_in(layer, h):
-        landed(two_slot(layer, 0, h, rest), two_sem.at[layer, 0, h])
-        landed(one_slot(layer, h, rest), one_sem.at[layer, h])
+    def columns_in(layer, h, wait):
+        if wait:
+            landed(two_slot(layer, 0, h, rest), two_sem.at[layer, 0, h])
+            landed(one_slot(layer, h, rest), one_sem.at[layer, h])
         return own_terms(layer, HERE, h) + [(two, two_at(layer, 0, h)), (one, one_at(layer, h))]
 
     def ways(reach, hop, leap):
@@ -394,26 +395,32 @@
             near, z_sem, c_sem = (low, low_sem, clow_sem) if name == "up" else (high, high_sem, chigh_sem)
             yield cond, to, name, over, joins, near, z_sem, c_sem
 
+    middle = split_back + (width - split_back) // (2 * TILE) * TILE
+    parts = (slice(split_back, middle), slice(middle, width))
+
     def z_sum(reach, hop, only=None):
         for h in (0, 1) if only is None else (only,):
             for cond, to, name, over, joins, near, sem, _ in ways(reach, hop, jump and h == 0):
-                def act():
-                    terms = columns_in(to, h)
-                    if joins:
-                        landed(near.at[pl.ds(post(to, HERE, h), half), rest], sem.at[to, h])
-                        terms.append((near, post(to, HERE, h)))
-                    add(half, rest, terms, mine, post(to, HERE, h))
-                pl.when(cond)(act)
-
-                def target(to=to, near=near, over=over, h=h):
-                    ref, at = (far, post(0, HERE, h)) if over else (near, post(to, HERE, h))
-                    return ref.at[pl.ds(at, half), rest]
-                send_sum(
-                    ("z sum", name, hop), lambda cond=cond: cond, lambda to=to: to, HERE, h, half,
-                    rest, target,
-                    lambda to=to, sem=sem, over=over, h=h: far_sem.at[h] if over else sem.at[to, h],
-                    lambda to=to, name=name, over=over: (
-                        (column(to), me.c) if over else device(name)))
+                for p, cols in enumerate(parts):
+                    def act():
+                        terms = columns_in(to, h, p == 0)
+                        if joins:
+                            landed(near.at[pl.ds(post(to, HERE, h), half), cols], sem.at[to, h, p])
+                            terms.append((near, post(to, HERE, h)))
+                        add(half, cols, terms, mine, post(to, HERE, h))
+                    pl.when(cond)(act)
+
+                    def target(to=to, near=near, over=over, h=h, cols=cols):
+                        ref, at = (far, post(0, HERE, h)) if over else (near, post(to, HERE, h))
+                        return ref.at[pl.ds(at, half), cols]
+                    send_sum(
+                        ("z sum", name, hop), lambda cond=cond: cond, lambda to=to: to, HERE, h, half,
+                        cols, target,
+                        lambda to=to, sem=sem, over=over, h=h, p=p: (
+                            far_sem.at[p] if over else sem.at[to, h, p]),
+                        lambda to=to, name=name, over=over: (
+                            (column(to), me.c) if over else device(name)),
+                        spent=(half if p else 0, rest))
 
     def c_sum(reach, hop):
         for cond, to, name, _, joins, near, _, sem in ways(reach, hop, False):
@@ -437,14 +444,15 @@
 
     def z_final():
         for h in range(2):
-            terms = columns_in(me.z, h)[2:] + lined(HERE, h, jump and h == 0)
             spot = pl.ds(post(me.z, HERE, h), half)
-            pl.when(me.below)(lambda: landed(low.at[spot, rest], low_sem.at[me.z, h]))
-            pl.when(me.above)(lambda: landed(high.at[spot, rest], high_sem.at[me.z, h]))
-            if jump and h == 0:
-                spot_far = pl.ds(post(0, HERE, h), half)
-                pl.when(me.end)(lambda: landed(far.at[spot_far, rest], far_sem.at[h]))
-            add(half, rest, terms, out_ref, h * half)
+            spot_far = pl.ds(post(0, HERE, h), half)
+            for p, cols in enumerate(parts):
+                terms = columns_in(me.z, h, p == 0)[2:] + lined(HERE, h, jump and h == 0)
+                pl.when(me.below)(lambda: landed(low.at[spot, cols], low_sem.at[me.z, h, p]))
+                pl.when(me.above)(lambda: landed(high.at[spot, cols], high_sem.at[me.z, h, p]))
+                if jump and h == 0:
+                    pl.when(me.end)(lambda: landed(far.at[spot_far, cols], far_sem.at[p]))
+                add(half, cols, terms, out_ref, h * half)
 
     def c_back():
         for flip in (DIAG,) + FLIPS + (HERE,):
@@ -616,7 +624,7 @@
             vmem(lined, width), vmem(lined, width),
             vmem(4 * rows, width),
             dma, dma((2,)), dma((experts,)), dma((groups,)), dma((2, columns)), dma((columns,)), dma((2,)),
-            dma((deep,)), dma((deep,)), dma((deep, 2, 2)), dma((deep, 2)), dma((deep, 2)), dma((deep, 2)),
+            dma((deep,)), dma((deep,)), dma((deep, 2, 2)), dma((deep, 2)), dma((deep, 2, 2)), dma((deep, 2, 2)),
             dma((2,)), dma((2, 2)), dma((2,)), dma((columns,)), dma((columns,)),
         ],
         compiler_params=pltpu.CompilerParams(

time: 72.8 us -> 72.4 us (level)
  no operation moved by 1% of the time
where the time goes in v5:
time: 72.4 us; the launch traced here: 72.2 us
  Pallas kernels  70.6 us (98%)
  local copies, waits for them, and re-layouts  1.64 us (2%)
    pallas_call x1, Pallas kernels, fused_body(): pl.pallas_call(functools.partial(layer_kernel, columns, split, split_back...  70.6 us
    unnamed x1, local copies, waits for them, and re-layouts  1.64 us

profile of v5, /device:TPU:0, one launch (start us, length us, event | category | flops | bytes accessed | tf_op | source)
XLA Modules:
  0.0 72.2 jit_solution(12049254179585491056)
XLA Ops:
  0.0 70.6 %expert_layer.1 = bf16[32,3584]{1,0:T(8,128)(2,1)} custom-call(bf16[32,3584]{1,0:T(8,128)(2,1)} %tokens_hbm.1, s32[8,32]{1,0:T(8,128)} %bitcast.2, bf16[8,32]{1,0:T(8,128)(2,1)} %bitcast.3, bf16[2,3584,512]{2,1,0:T(8,128)(2,1)} %wg_hbm.1, bf16[2,3584,512]{2,1,0:T(8,128)(2,1)} %wu_hbm.1, bf16[2,3584,512]{2,1,0:T(8,128)(2,1)} %wd_hbm.1), custom_call_target="tpu_custom_call" | custom-call | tf_op jit(solution)/shard_map/expert_layer/pallas_call | solution.py:610
  70.6 1.6 %copy.8 = bf16[32,3584]{1,0:T(8,128)(2,1)} copy(bf16[32,3584]{1,0:T(8,128)(2,1)} %expert_layer.1) | data formatting | bytes 458752
